TPU v7x, 128 devices: a whole 4x4x4 slice. The times are simulated.
128 devices in a mesh: bx: 4 (over z_hi, core), by: 8 (over z_lo, x), bz: 4 (over y).
Axes of the slice: x: 4, y: 4, z: 4 (z_hi: 2, z_lo: 2; z = z_hi * 2 + z_lo), core: 2. Of those that a mesh axis runs over, the one named last changes fastest.
Arguments:
- estimate: float32 [64, 128, 512], P('bx', 'by', 'bz'), may hold values from 0.2 to 5
- observed: float32 [8, 64, 128, 512], P(None, 'bx', 'by', 'bz'), may hold values from 0.3 to 180, as said below
- coverage: int32 [8, 4, 8, 4], P(None, 'bx', 'by', 'bz'), may hold values from 0 to 1, as said below
- psf_taps: float32 [8, 3, 17], replicated, may hold values from 0.05 to 1
Outputs:
- refined: float32 [64, 128, 512], P('bx', 'by', 'bz')
Inputs may be any that keep to these rules, and one draw needn't show every extreme that they name: `coverage`: each block is covered by 2 to 8 views; in every draw some block is covered by all 8. `observed`: positive.
All inputs are finite; a program needn't handle non-finite values.
Results may differ from a plain program's by a relative error of at most 0.0001.
Values sent between devices are 32-bit elements; how exact they have to be, the bound alone decides.
A program may use at most 64 MiB of HBM per device.

v0:
```python
import functools

import jax
import jax.numpy as jnp
from jax import lax
from jax.experimental import pallas as pl
from jax.experimental.pallas import tpu as pltpu
from jax.sharding import PartitionSpec as P

MESH = pl.DeviceIdType.MESH
F32 = jnp.float32
BF16 = jnp.bfloat16
V, R, T = 8, 8, 17
CX, CY, CZ = 16, 16, 128
EX, EY = CX + 2 * R, CY + 2 * R
LINES = (("bz", 4), ("by", 8), ("bx", 4))


def split(f):
    hi = f.astype(BF16)
    lo = (f - hi.astype(F32)).astype(BF16)
    return hi, lo


def dot(a, b):
    return jnp.dot(a, b, preferred_element_type=F32)


def stack4(f):
    hi, lo = split(f)
    return jnp.concatenate([hi, lo, hi, lo], axis=0)


def flip_tiles(f):
    return jnp.concatenate([f[:128].T, f[128:].T], axis=1)


def kernel(
    est, obs, cov, taps_s, taps_v, out,
    e_buf, o_buf, y_buf, g_buf, r_buf, x_buf, p_buf, rx_buf, ry_buf,
    sf_buf, hf_buf, sb_buf, hb_buf, w_buf, t_buf,
    zf_mat, zb_mat, yf_mat, yb_mat, red_own, red_in,
    load_sem, y_send, y_recv, x_send, x_recv, w_send, w_recv,
    zf_send, zf_recv, zb_send, zb_recv, rx_send, rx_recv, ry_send, ry_recv,
    red_send, red_recv,
):
    ids = {name: lax.axis_index(name) for name, _ in LINES}
    sizes = dict(LINES)

    barrier = pltpu.get_barrier_semaphore()
    for name, n in LINES:
        for d in range(1, n):
            pl.semaphore_signal(
                barrier, inc=1, device_id={name: lax.rem(ids[name] + d, n)}, device_id_type=MESH
            )
    load_e = pltpu.make_async_copy(est, e_buf.at[pl.ds(R, CX), pl.ds(R, CY)], load_sem.at[0])
    load_o = pltpu.make_async_copy(obs, o_buf, load_sem.at[1])
    load_e.start()
    load_o.start()

    def has(name, side):
        return ids[name] > 0 if side == 0 else ids[name] < sizes[name] - 1

    def peer(name, side):
        return {name: ids[name] - 1 if side == 0 else ids[name] + 1}

    def remote(src, dst, send, recv, name, side):
        return pltpu.make_async_remote_copy(
            src_ref=src, dst_ref=dst, send_sem=send, recv_sem=recv,
            device_id=peer(name, side), device_id_type=MESH,
        )

    edge = (pl.ds(0, R), pl.ds(EX - R, R))
    inner = (pl.ds(R, R), pl.ds(CX, R))

    def y_copy(side):
        return remote(
            e_buf.at[pl.ds(R, CX), inner[side]], e_buf.at[pl.ds(R, CX), edge[1 - side]],
            y_send.at[side], y_recv.at[1 - side], "by", side,
        )

    def yw_copy(side):
        return remote(
            w_buf.at[1, 1], w_buf.at[1, 2 - 2 * side],
            w_send.at[0, side], w_recv.at[0, 1 - side], "by", side,
        )

    def x_copy(side):
        return remote(
            e_buf.at[inner[side]], e_buf.at[edge[1 - side]],
            x_send.at[side], x_recv.at[1 - side], "bx", side,
        )

    def xw_copy(side):
        return remote(
            w_buf.at[1], w_buf.at[2 - 2 * side],
            w_send.at[1, side], w_recv.at[1, 1 - side], "bx", side,
        )

    def zf_copy(v, side):
        return remote(
            sf_buf.at[v, pl.ds(R - R * side, R)], hf_buf.at[v, pl.ds(R * side, R)],
            zf_send.at[v, side], zf_recv.at[v, 1 - side], "bz", side,
        )

    def zb_copy(v, side):
        return remote(
            sb_buf.at[v, pl.ds(R - R * side, R)], hb_buf.at[v, pl.ds(R * side, R)],
            zb_send.at[v, side], zb_recv.at[v, 1 - side], "bz", side,
        )

    def rx_copy(side):
        return remote(
            p_buf.at[edge[side]], rx_buf.at[1 - side],
            rx_send.at[side], rx_recv.at[1 - side], "bx", side,
        )

    def ry_copy(side):
        return remote(
            p_buf.at[pl.ds(R, CX), edge[side]], ry_buf.at[1 - side],
            ry_send.at[side], ry_recv.at[1 - side], "by", side,
        )

    def start(copies, name):
        for side in (0, 1):
            @pl.when(has(name, side))
            def _():
                for c in copies:
                    c(side).start()

    def finish(copies, name):
        for side in (0, 1):
            @pl.when(has(name, side))
            def _():
                for c in copies:
                    c(side).wait_send()
                    c(1 - side).wait_recv()

    for side in (0, 1):
        @pl.when(jnp.logical_not(has("by", side)))
        def _():
            e_buf[R:R + CX, edge[side], :] = jnp.zeros((CX, R, CZ), F32)
            w_buf[1, 2 * side] = jnp.zeros((V, CZ), F32)
            ry_buf[side] = jnp.zeros((CX, R, CZ), F32)

        @pl.when(jnp.logical_not(has("bx", side)))
        def _():
            e_buf[edge[side]] = jnp.zeros((R, EY, CZ), F32)
            w_buf[2 * side] = jnp.zeros((3, V, CZ), F32)
            rx_buf[side] = jnp.zeros((R, EY, CZ), F32)

        @pl.when(jnp.logical_not(has("bz", side)))
        def _():
            rows = pl.ds(R - R * side, R)
            hf_buf[:, rows, :] = jnp.zeros((V, R, CX * CY), F32)
            hb_buf[:, rows, :] = jnp.zeros((V, R, CX * CY), F32)

    row8 = lax.broadcasted_iota(jnp.int32, (V, CZ), 0)
    weight = jnp.zeros((V, CZ), F32)
    for v in range(V):
        weight = weight + jnp.where(row8 == v, cov[v, 0, 0, 0].astype(F32), 0.0)
    w_buf[1, 1] = weight

    load_e.wait()
    pl.semaphore_wait(barrier, sum(n - 1 for _, n in LINES))
    start((y_copy, yw_copy), "by")

    t_buf[...] = jnp.zeros_like(t_buf)
    t_buf[:, 0:3, 0:T] = taps_v[...]

    lane = lax.broadcasted_iota(jnp.int32, (128, 128), 1)
    row = lax.broadcasted_iota(jnp.int32, (128, 128), 0)
    near = jnp.abs(row - lane) <= R
    band = lax.broadcasted_iota(jnp.int32, (CY, 128), 1)
    zf_mat[...] = jnp.zeros_like(zf_mat)
    zb_mat[...] = jnp.zeros_like(zb_mat)

    def build(v, carry):
        sums = jnp.sum(t_buf[v], axis=1, keepdims=True)
        ty = t_buf[v, 1:2, :] / sums[1:2]
        tz = t_buf[v, 2:3, :] / (sums[2:3] * sums[0:1])
        ty = ty + pltpu.roll(ty, 32, 1)
        ty = ty + pltpu.roll(ty, 64, 1)
        q = pltpu.roll(jnp.broadcast_to(ty, (CY, 128)), 0, 1, stride=1, stride_axis=0)
        q_hi, q_lo = split(q)
        zero = jnp.zeros_like(q_hi)
        for x in range(2):
            mine = (band // 32) % 2 == x
            yf_mat[v, x * CY:(x + 1) * CY, 0:128] = jnp.where(mine, q_hi, zero)
            yf_mat[v, x * CY:(x + 1) * CY, 128:256] = jnp.where(mine, q_lo, zero)
        q4 = jnp.concatenate(
            [jnp.where(band // 32 == x % 4, q, 0.0) for x in range(8)], axis=0
        ).T
        b_hi, b_lo = split(q4)
        yb_mat[v, :, 0:128] = b_hi
        yb_mat[v, :, 128:256] = b_lo

        ring = pltpu.roll(jnp.broadcast_to(tz, (128, 128)), 128 - R, 1, stride=1, stride_axis=0)
        for mat, full in ((zb_mat, ring), (zf_mat, ring.T)):
            m_hi, m_lo = split(jnp.where(near, full, 0.0))
            mat[v, 0:128, 0:128] = m_hi
            mat[v, 0:128, 128:256] = m_lo
            far = jnp.where(near, 0.0, full)
            far = jnp.concatenate([far[0:R], far[128 - R:128]], axis=0)
            f_hi, f_lo = split(far)
            rows = pl.ds(pl.multiple_of(128 + 2 * R * v, 2 * R), 2 * R)
            mat[v, rows, 0:128] = f_hi
            mat[v, rows, 128:256] = f_lo
        return carry

    lax.fori_loop(0, V, build, 0)

    finish((y_copy, yw_copy), "by")
    start((x_copy, xw_copy), "bx")

    def forward_y(x0):
        data = jnp.concatenate(
            [stack4(e_buf[pl.ds(x0 + 2 * h, 2)].reshape(2 * EY, CZ)) for h in range(2)], axis=1
        )
        full = dot(yf_mat[...].reshape(V * 2 * CY, 256), data)
        for h in range(2):
            y_buf[:, pl.ds(x0 + 2 * h, 2)] = full[:, h * CZ:(h + 1) * CZ].reshape(V, 2, CY, CZ)

    for x0 in range(R, R + CX, 4):
        forward_y(x0)

    load_o.wait()
    seen = jnp.zeros((8, CZ), F32)
    for v in range(V):
        seen = seen + w_buf[1, 1, v:v + 1, :] * jnp.sum(o_buf[v].reshape(CX * CY // 8, 8, CZ), axis=0)
    count_own = jnp.sum(w_buf[1, 1], axis=0, keepdims=True)
    red_own[0] = seen / count_own

    finish((x_copy, xw_copy), "bx")
    for x0 in (0, 4, EX - 8, EX - 4):
        forward_y(x0)

    def forward_x(v, carry):
        t = [jnp.full((8, CZ), taps_s[v, 0, k], F32) for k in range(T)]
        for h in range(CY // 8):
            ys = pl.ds(8 * h, 8)
            acc = [None] * CX
            for xi in range(EX):
                val = y_buf[v, xi, ys, :]
                for xo in range(max(0, xi - T + 1), min(CX, xi + 1)):
                    term = t[xi - xo] * val
                    acc[xo] = term if acc[xo] is None else acc[xo] + term
                if xi >= T - 1:
                    g_buf[v, xi - T + 1, ys, :] = acc[xi - T + 1]
        flipped = flip_tiles(g_buf[v].reshape(CX * CY, CZ))
        sf_buf[v, 0:R] = flipped[CZ - R:]
        sf_buf[v, R:2 * R] = flipped[:R]
        start((functools.partial(zf_copy, v),), "bz")
        return carry

    lax.fori_loop(0, V, forward_x, 0)

    def halo_rows(h_buf):
        flat = h_buf[...].reshape(V * 2 * R, CX * CY)
        return split(jnp.concatenate([flat[:, :128].T, flat[:, 128:].T], axis=0))

    def z_apply(f, halo, mat, v):
        hi, lo = split(f)
        both = dot(jnp.concatenate([hi, halo[0]], axis=1), mat[v])
        rest = dot(jnp.concatenate([lo, halo[1]], axis=1), mat[v, :, 0:128])
        return both[:, :128] + both[:, 128:] + rest

    for v in range(V):
        finish((functools.partial(zf_copy, v),), "bz")
    halo = halo_rows(hf_buf)
    for v in range(V):
        blurred = z_apply(g_buf[v].reshape(CX * CY, CZ), halo, zf_mat, v)
        ratio = o_buf[v].reshape(CX * CY, CZ) / blurred
        r_buf[v] = ratio.reshape(CX, CY, CZ)
        flipped = flip_tiles(ratio)
        sb_buf[v, 0:R] = flipped[CZ - R:]
        sb_buf[v, R:2 * R] = flipped[:R]
        start((functools.partial(zb_copy, v),), "bz")

    for v in range(V):
        finish((functools.partial(zb_copy, v),), "bz")
    halo = halo_rows(hb_buf)
    for v in range(V):
        f = r_buf[v].reshape(CX * CY, CZ)
        g_buf[v] = z_apply(f, halo, zb_mat, v).reshape(CX, CY, CZ)

    def backward_x(v, carry):
        t = [jnp.full((8, CZ), taps_s[v, 0, k], F32) for k in range(T)]
        for h in range(CY // 8):
            ys = pl.ds(8 * h, 8)
            val = [g_buf[v, xi, ys, :] for xi in range(CX)]
            for xo in range(EX):
                acc = None
                for xi in range(max(0, xo - T + 1), min(CX, xo + 1)):
                    term = t[xo - xi] * val[xi]
                    acc = term if acc is None else acc + term
                x_buf[v, xo, ys, :] = acc
        return carry

    lax.fori_loop(0, V, backward_x, 0)

    def backward_y(x0, xb):
        def one(v, acc):
            data = jnp.concatenate(
                [stack4(x_buf[v, pl.ds(x0 + 4 * h, 4)].reshape(4 * CY, CZ)) for h in range(2)], axis=1
            )
            full = dot(yb_mat[v], data)
            new = []
            for h in range(2):
                part = full[:, h * CZ:(h + 1) * CZ].reshape(4, EY, CZ)
                for x in range(4):
                    for t in range(4):
                        w = w_buf[xb, (0, 1, 1, 2)[t], pl.ds(v, 1), :]
                        new.append(w * part[x, 8 * t:8 * t + 8])
            return tuple(a + b for a, b in zip(acc, new))

        acc = lax.fori_loop(0, V, one, tuple(jnp.zeros((8, CZ), F32) for _ in range(32)))
        for x in range(8):
            for t in range(4):
                p_buf[x0 + x, 8 * t:8 * t + 8, :] = acc[4 * x + t]

    backward_y(0, 0)
    backward_y(EX - 8, 2)
    start((rx_copy,), "bx")
    backward_y(R, 1)
    backward_y(2 * R, 1)

    total = jnp.zeros((8, CZ), F32)
    for xb, xs in ((0, range(0, R)), (1, range(R, R + CX)), (2, range(R + CX, EX))):
        for yb, ys in ((0, (0,)), (1, (1, 2)), (2, (3,))):
            count = jnp.maximum(jnp.sum(w_buf[xb, yb], axis=0, keepdims=True), 1.0)
            part = jnp.zeros((8, CZ), F32)
            for x in xs:
                for t in ys:
                    part = part + e_buf[x, 8 * t:8 * t + 8, :] * p_buf[x, 8 * t:8 * t + 8, :]
            total = total + part / count
    red_own[1] = total
    red_own[0] = jnp.where(
        row8 == 0, jnp.sum(red_own[0], axis=0, keepdims=True),
        jnp.where(row8 == 1, jnp.sum(total, axis=0, keepdims=True), 0.0),
    )

    def red_copy(stage, d):
        name, n = LINES[stage]
        return pltpu.make_async_remote_copy(
            src_ref=red_own.at[0 if stage == 0 else stage + 1], dst_ref=red_in.at[stage, d],
            send_sem=red_send.at[stage, d], recv_sem=red_recv.at[stage, d],
            device_id={name: lax.rem(ids[name] + d, n)}, device_id_type=MESH,
        )

    def red_start(stage):
        for d in range(1, LINES[stage][1]):
            red_copy(stage, d).start()

    def red_finish(stage):
        total = red_own[0 if stage == 0 else stage + 1]
        for d in range(1, LINES[stage][1]):
            red_copy(stage, d).wait()
            total = total + red_in[stage, d]
        red_own[stage + 2] = total

    red_start(0)
    red_finish(0)
    red_start(1)

    finish((rx_copy,), "bx")
    p_buf[R:2 * R] = p_buf[R:2 * R] + rx_buf[0]
    p_buf[2 * R:3 * R] = p_buf[2 * R:3 * R] + rx_buf[1]
    start((ry_copy,), "by")
    red_finish(1)
    red_start(2)
    red_finish(2)
    final = red_own[4]
    scale = jnp.sum(final[0:1], axis=1, keepdims=True) / (
        jnp.sum(final[1:2], axis=1, keepdims=True) * count_own[:, 0:1]
    )
    finish((ry_copy,), "by")
    for h in range(2):
        ys = slice(R + 8 * h, R + 8 * h + 8)
        summed = p_buf[R:R + CX, ys, :] + ry_buf[h]
        out[:, 8 * h:8 * h + 8, :] = e_buf[R:R + CX, ys, :] * summed * scale.reshape(1, 1, 1)


def on_device(estimate, observed, coverage, psf_taps):
    dma = pltpu.SemaphoreType.DMA
    return pl.pallas_call(
        kernel,
        out_shape=jax.ShapeDtypeStruct((CX, CY, CZ), F32),
        in_specs=[
            pl.BlockSpec(memory_space=pl.ANY),
            pl.BlockSpec(memory_space=pl.ANY),
            pl.BlockSpec(memory_space=pltpu.SMEM),
            pl.BlockSpec(memory_space=pltpu.SMEM),
            pl.BlockSpec(memory_space=pltpu.VMEM),
        ],
        out_specs=pl.BlockSpec(memory_space=pltpu.VMEM),
        scratch_shapes=[
            pltpu.VMEM((EX, EY, CZ), F32),
            pltpu.VMEM((V, CX, CY, CZ), F32),
            pltpu.VMEM((V, EX, CY, CZ), F32),
            pltpu.VMEM((V, CX, CY, CZ), F32),
            pltpu.VMEM((V, CX, CY, CZ), F32),
            pltpu.VMEM((V, EX, CY, CZ), F32),
            pltpu.VMEM((EX, EY, CZ), F32),
            pltpu.VMEM((2, R, EY, CZ), F32),
            pltpu.VMEM((2, CX, R, CZ), F32),
            pltpu.VMEM((V, 2 * R, CX * CY), F32),
            pltpu.VMEM((V, 2 * R, CX * CY), F32),
            pltpu.VMEM((V, 2 * R, CX * CY), F32),
            pltpu.VMEM((V, 2 * R, CX * CY), F32),
            pltpu.VMEM((3, 3, V, CZ), F32),
            pltpu.VMEM((V, 8, 128), F32),
            pltpu.VMEM((V, 256, 256), BF16),
            pltpu.VMEM((V, 256, 256), BF16),
            pltpu.VMEM((V, 2 * CY, 256), BF16),
            pltpu.VMEM((V, 128, 256), BF16),
            pltpu.VMEM((5, 8, CZ), F32),
            pltpu.VMEM((3, 8, 8, CZ), F32),
            dma((2,)), dma((2,)), dma((2,)), dma((2,)), dma((2,)), dma((2, 2)), dma((2, 2)),
            dma((V, 2)), dma((V, 2)), dma((V, 2)), dma((V, 2)), dma((2,)), dma((2,)), dma((2,)), dma((2,)),
            dma((3, 8)), dma((3, 8)),
        ],
        compiler_params=pltpu.CompilerParams(
            collective_id=0, has_side_effects=True, vmem_limit_bytes=48 * 1024 * 1024
        ),
    )(estimate, observed, coverage, psf_taps, psf_taps)


def solution(mesh):
    block = P("bx", "by", "bz")
    views = P(None, "bx", "by", "bz")
    return jax.shard_map(
        on_device, mesh=mesh, in_specs=(block, views, views, P()), out_specs=block, check_vma=False
    )
```

profile of v0, /device:TPU:1, one launch (start us, length us, event | category | flops | bytes accessed | tf_op | source)
XLA Modules:
  0.0 50.6 jit_solution(17899667117553683586)
XLA Ops:
  0.0 0.7 %copy.5.cov = s32[8,1,1,1]{3,2,1,0:T(1,128)S(1)} copy(s32[8,1,1,1]{0,3,2,1:T(1,128)} %param.6) | data formatting | bytes 64 | tf_op args[2]
  0.7 0.7 %copy.6.taps_s.taps_v = f32[8,3,17]{2,1,0:T(4,128)S(1)} copy(f32[8,3,17]{2,0,1:T(8,128)} %param.7) | data formatting | bytes 3264 | tf_op args[3]
  1.4 0.0 copy-start
  1.4 1.2 %copy-done = f32[8,16,16,128]{3,2,1,0:T(8,128)S(1)} copy-done((f32[8,16,16,128]{3,2,1,0:T(8,128)S(1)}, f32[8,16,16,128]{3,2,1,0:T(8,128)}, u32[]{:S(2)}) %copy-start) | copy-done | bytes 1048600
  2.7 0.0 copy-start.1
  2.7 0.9 %copy-done.1 = f32[16,16,128]{2,1,0:T(8,128)S(1)} copy-done((f32[16,16,128]{2,1,0:T(8,128)S(1)}, f32[16,16,128]{2,1,0:T(8,128)}, u32[]{:S(2)}) %copy-start.1) | copy-done | bytes 131096
  3.6 46.4 %shard_map.46 = f32[16,16,128]{2,1,0:T(8,128)S(1)} custom-call(f32[16,16,128]{2,1,0:T(8,128)S(1)} %copy-done.1, f32[8,16,16,128]{3,2,1,0:T(8,128)S(1)} %copy-done, s32[8,1,1,1]{3,2,1,0:T(1,128)S(1)} %copy.5.cov, f32[8,3,17]{2,1,0:T(4,128)S(1)} %copy.6.taps_s.taps_v, f32[8,3,17]{2,1,0:T(4,128)S(1)} %copy.6.taps_s.taps_v), custom_call_target="tpu_custom_call" | custom-call | tf_op jit(solution)/shard_map/pallas_call | solution.py:386
  49.9 0.7 %copy.9 = f32[16,16,128]{2,1,0:T(8,128)} copy(f32[16,16,128]{2,1,0:T(8,128)S(1)} %shard_map.46) | data formatting | bytes 262144
Async XLA Ops:
  1.4 1.2 %copy-start = (f32[8,16,16,128]{3,2,1,0:T(8,128)S(1)}, f32[8,16,16,128]{3,2,1,0:T(8,128)}, u32[]{:S(2)}) copy-start(f32[8,16,16,128]{3,2,1,0:T(8,128)} %obs.1) | copy-start | bytes 3145732
  2.7 0.9 %copy-start.1 = (f32[16,16,128]{2,1,0:T(8,128)S(1)}, f32[16,16,128]{2,1,0:T(8,128)}, u32[]{:S(2)}) copy-start(f32[16,16,128]{2,1,0:T(8,128)} %est.1) | copy-start | bytes 393220
where the time goes:
time: 50.8 us; the launch traced here: 50.6 us
  Pallas kernels  46.4 us (91%)
  local copies, waits for them, and re-layouts  4.23 us (8%)
    pallas_call x1, Pallas kernels, on_device(): pl.pallas_call(kernel, out_shape=jax.ShapeDtypeStruct((CX, CY, CZ), F32),...  46.4 us
    unnamed x7, local copies, waits for them, and re-layouts  4.23 us

commit v1 on v0

v1 whole, which is shorter than its diff:
```python
import functools

import jax
import jax.numpy as jnp
from jax import lax
from jax.experimental import pallas as pl
from jax.experimental.pallas import tpu as pltpu
from jax.sharding import PartitionSpec as P

MESH = pl.DeviceIdType.MESH
F32 = jnp.float32
BF16 = jnp.bfloat16
V, R, T = 8, 8, 17
CX, CY, CZ = 16, 16, 128
EX, EY = CX + 2 * R, CY + 2 * R
G = 4
LINES = (("bz", 4), ("by", 8), ("bx", 4))


def split(f):
    hi = f.astype(BF16)
    lo = (f - hi.astype(F32)).astype(BF16)
    return hi, lo


def dot(a, b):
    return jnp.dot(a, b, preferred_element_type=F32)


def stack4(f):
    hi, lo = split(f)
    return jnp.concatenate([hi, lo, hi, lo], axis=0)


def kernel(
    est, obs, cov, taps, out,
    e_buf, o_buf, y_buf, g_buf, r_buf, x_buf, p_buf, rx_buf, ry_buf,
    sf_buf, hf_buf, sb_buf, hb_buf, w_buf, c_buf, k_buf, t_buf,
    zf_mat, zb_mat, yf_mat, yb_mat, red_own, red_in,
    load_sem, y_send, y_recv, x_send, x_recv, w_send, w_recv,
    zf_send, zf_recv, zb_send, zb_recv, rx_send, rx_recv, ry_send, ry_recv,
    red_send, red_recv,
):
    ids = {name: lax.axis_index(name) for name, _ in LINES}
    sizes = dict(LINES)

    barrier = pltpu.get_barrier_semaphore()
    for name, n in LINES:
        for d in range(1, n):
            pl.semaphore_signal(
                barrier, inc=1, device_id={name: lax.rem(ids[name] + d, n)}, device_id_type=MESH
            )
    load_e = pltpu.make_async_copy(est, e_buf.at[pl.ds(R, CX), pl.ds(R, CY)], load_sem.at[0])
    load_c = pltpu.make_async_copy(cov, c_buf, load_sem.at[1])
    load_t = pltpu.make_async_copy(taps, k_buf, load_sem.at[2])
    load_o = pltpu.make_async_copy(obs, o_buf, load_sem.at[3])
    for load in (load_e, load_c, load_t, load_o):
        load.start()

    def has(name, side):
        return ids[name] > 0 if side == 0 else ids[name] < sizes[name] - 1

    def peer(name, side):
        return {name: ids[name] - 1 if side == 0 else ids[name] + 1}

    def remote(src, dst, send, recv, name, side):
        return pltpu.make_async_remote_copy(
            src_ref=src, dst_ref=dst, send_sem=send, recv_sem=recv,
            device_id=peer(name, side), device_id_type=MESH,
        )

    edge = (pl.ds(0, R), pl.ds(EX - R, R))
    inner = (pl.ds(R, R), pl.ds(CX, R))
    own = pl.ds(R, CX)
    y_parts = (own, edge[0], edge[1])

    def y_copy(side):
        return remote(
            e_buf.at[own, inner[side]], e_buf.at[own, edge[1 - side]],
            y_send.at[side], y_recv.at[1 - side], "by", side,
        )

    def yw_copy(side):
        return remote(
            w_buf.at[1, 1], w_buf.at[1, 2 - 2 * side],
            w_send.at[0, side], w_recv.at[0, 1 - side], "by", side,
        )

    def x_copy(part, side):
        return remote(
            e_buf.at[inner[side], y_parts[part]], e_buf.at[edge[1 - side], y_parts[part]],
            x_send.at[part, side], x_recv.at[part, 1 - side], "bx", side,
        )

    def xw_copy(side):
        return remote(
            w_buf.at[1], w_buf.at[2 - 2 * side],
            w_send.at[1, side], w_recv.at[1, 1 - side], "bx", side,
        )

    def z_copy(s_buf, h_buf, send, recv, g, side):
        views = pl.ds(G * g, G)
        return remote(
            s_buf.at[views, pl.ds(R - R * side, R)], h_buf.at[views, pl.ds(R * side, R)],
            send.at[g, side], recv.at[g, 1 - side], "bz", side,
        )

    def rx_copy(part, side):
        return remote(
            p_buf.at[edge[side], y_parts[part]], rx_buf.at[1 - side, :, y_parts[part]],
            rx_send.at[part, side], rx_recv.at[part, 1 - side], "bx", side,
        )

    def ry_copy(side):
        return remote(
            p_buf.at[own, edge[side]], ry_buf.at[1 - side],
            ry_send.at[side], ry_recv.at[1 - side], "by", side,
        )

    def start(copies, name):
        for side in (0, 1):
            @pl.when(has(name, side))
            def _():
                for c in copies:
                    c(side).start()

    def finish(copies, name):
        for side in (0, 1):
            @pl.when(has(name, side))
            def _():
                for c in copies:
                    c(1 - side).wait_recv()
                    c(side).wait_send()

    part = functools.partial
    x_first = (part(x_copy, 0),)
    x_second = (part(x_copy, 1), part(x_copy, 2), xw_copy)

    for side in (0, 1):
        @pl.when(jnp.logical_not(has("by", side)))
        def _():
            e_buf[R:R + CX, edge[side], :] = jnp.zeros((CX, R, CZ), F32)
            w_buf[1, 2 * side] = jnp.zeros((V, CZ), F32)
            ry_buf[side] = jnp.zeros((CX, R, CZ), F32)

        @pl.when(jnp.logical_not(has("bx", side)))
        def _():
            e_buf[edge[side]] = jnp.zeros((R, EY, CZ), F32)
            w_buf[2 * side] = jnp.zeros((3, V, CZ), F32)
            rx_buf[side] = jnp.zeros((R, EY, CZ), F32)

        @pl.when(jnp.logical_not(has("bz", side)))
        def _():
            rows = pl.ds(R - R * side, R)
            hf_buf[:, rows, :] = jnp.zeros((V, R, CX * CY), F32)
            hb_buf[:, rows, :] = jnp.zeros((V, R, CX * CY), F32)

    row8 = lax.broadcasted_iota(jnp.int32, (V, CZ), 0)
    lane8 = lax.broadcasted_iota(jnp.int32, (V, CZ), 1)
    load_c.wait()
    flags = jnp.broadcast_to(c_buf[...].astype(F32), (V, V))
    picked = jnp.where(row8[:, :V] == lane8[:, :V], flags, 0.0)
    w_buf[1, 1] = jnp.broadcast_to(jnp.sum(picked, axis=1, keepdims=True), (V, CZ))
    load_e.wait()
    pl.semaphore_wait(barrier, sum(n - 1 for _, n in LINES))
    start((y_copy, yw_copy), "by")
    start(x_first, "bx")

    load_t.wait()
    t_buf[...] = jnp.zeros_like(t_buf)
    for d in range(3):
        t_buf[d, :, 0:T] = k_buf[d]
    taps_x, taps_y, taps_z = (
        t_buf[d] / jnp.sum(t_buf[d], axis=1, keepdims=True) for d in range(3)
    )
    taps_y = taps_y + pltpu.roll(taps_y, 32, 1)
    taps_y = taps_y + pltpu.roll(taps_y, 64, 1)
    band = lax.broadcasted_iota(jnp.int32, (CY, 128), 1)
    bands = []
    for v in range(V):
        q = pltpu.roll(
            jnp.broadcast_to(taps_y[v:v + 1], (CY, 128)), 0, 1, stride=1, stride_axis=0
        )
        bands.append(q)
        q_hi, q_lo = split(q)
        zero = jnp.zeros_like(q_hi)
        for x in range(2):
            mine = (band // 32) % 2 == x
            yf_mat[v, x * CY:(x + 1) * CY, 0:128] = jnp.where(mine, q_hi, zero)
            yf_mat[v, x * CY:(x + 1) * CY, 128:256] = jnp.where(mine, q_lo, zero)
    for k in range(T):
        t_buf[3 + k] = jnp.broadcast_to(taps_x[:, k:k + 1], (V, CZ))

    finish((y_copy, yw_copy), "by")
    start(x_second, "bx")

    def forward_y(x0):
        data = jnp.concatenate(
            [stack4(e_buf[pl.ds(x0 + 2 * h, 2)].reshape(2 * EY, CZ)) for h in range(2)], axis=1
        )
        full = dot(yf_mat[...].reshape(V * 2 * CY, 256), data)
        for h in range(2):
            y_buf[:, pl.ds(x0 + 2 * h, 2)] = full[:, h * CZ:(h + 1) * CZ].reshape(V, 2, CY, CZ)

    for x0 in range(R, R + CX, 4):
        forward_y(x0)

    def x_taps(v):
        return [jnp.broadcast_to(t_buf[3 + k, pl.ds(v, 1), :], (8, CZ)) for k in range(T)]

    def forward_x(inputs, first, v, carry):
        t = x_taps(v)
        for h in range(CY // 8):
            ys = pl.ds(8 * h, 8)
            acc = [None if first else g_buf[v, xo, ys, :] for xo in range(CX)]
            for xi in inputs:
                val = y_buf[v, xi, ys, :]
                for xo in range(max(0, xi - T + 1), min(CX, xi + 1)):
                    term = t[xi - xo] * val
                    acc[xo] = term if acc[xo] is None else acc[xo] + term
            for xo in range(CX):
                g_buf[v, xo, ys, :] = acc[xo]
        return carry

    lax.fori_loop(0, V, part(forward_x, range(R, R + CX), True), 0)

    lane = lax.broadcasted_iota(jnp.int32, (128, 128), 1)
    row = lax.broadcasted_iota(jnp.int32, (128, 128), 0)
    near = jnp.abs(row - lane) <= R
    for mat in (zf_mat, zb_mat):
        mat[:, 128:192, :] = jnp.zeros((V, 64, 256), BF16)
    for v in range(V):
        ring = pltpu.roll(
            jnp.broadcast_to(taps_z[v:v + 1], (128, 128)), 128 - R, 1, stride=1, stride_axis=0
        )
        for mat, full in ((zb_mat, ring), (zf_mat, ring.T)):
            m_hi, m_lo = split(jnp.where(near, full, 0.0))
            mat[v, 0:128, 0:128] = m_hi
            mat[v, 0:128, 128:256] = m_lo
            far = jnp.where(near, 0.0, full)
            far = jnp.concatenate([far[0:R], far[128 - R:128]], axis=0)
            f_hi, f_lo = split(far)
            at = 128 + 2 * R * (v % G)
            mat[v, at:at + 2 * R, 0:128] = f_hi
            mat[v, at:at + 2 * R, 128:256] = f_lo

    load_o.wait()
    seen = jnp.zeros((8, CZ), F32)
    for v in range(V):
        seen = seen + w_buf[1, 1, v:v + 1, :] * jnp.sum(o_buf[v].reshape(CX * CY // 8, 8, CZ), axis=0)
    count_own = jnp.sum(w_buf[1, 1], axis=0, keepdims=True)
    red_own[1] = seen / count_own

    finish(x_first + x_second, "bx")
    for x0 in (0, 4, EX - 8, EX - 4):
        forward_y(x0)

    def send_edges(fields, s_buf, h_buf, send, recv, g):
        for v, f in zip(range(G * g, G * g + G), fields):
            for h in range(2):
                flipped = f[128 * h:128 * h + 128].T
                s_buf[v, 0:R, 128 * h:128 * h + 128] = flipped[CZ - R:]
                s_buf[v, R:2 * R, 128 * h:128 * h + 128] = flipped[:R]
        start((part(z_copy, s_buf, h_buf, send, recv, g),), "bz")

    def halo_rows(h_buf, g):
        flat = h_buf[G * g:G * g + G].reshape(G * 2 * R, CX * CY)
        return split(jnp.concatenate([flat[:, :128].T, flat[:, 128:].T], axis=0))

    def z_apply(f, halo, mat, v):
        hi, lo = split(f)
        both = dot(jnp.concatenate([hi, halo[0]], axis=1), mat[v])
        rest = dot(jnp.concatenate([lo, halo[1]], axis=1), mat[v, :, 0:128])
        return both[:, :128] + both[:, 128:] + rest

    forward = (sf_buf, hf_buf, zf_send, zf_recv)
    backward = (sb_buf, hb_buf, zb_send, zb_recv)
    halo_planes = tuple(range(R)) + tuple(range(R + CX, EX))
    for g in range(V // G):
        lax.fori_loop(G * g, G * g + G, part(forward_x, halo_planes, False), 0)
        send_edges(
            [g_buf[v].reshape(CX * CY, CZ) for v in range(G * g, G * g + G)], *forward, g
        )

    for v in range(V):
        q4 = jnp.concatenate(
            [jnp.where(band // 32 == i // 2, bands[v], 0.0) for i in range(8)], axis=0
        ).T
        both = split(q4)
        for xb in range(3):
            w = [jnp.broadcast_to(w_buf[xb, yb, v:v + 1, :], (8, CZ)) for yb in (0, 1, 1, 2)]
            w = jnp.concatenate(w * 4, axis=0).astype(BF16)
            for i in range(2):
                yb_mat[xb, v, :, 128 * i:128 * i + 128] = both[i] * w

    for g in range(V // G):
        finish((part(z_copy, *forward, g),), "bz")
        halo = halo_rows(hf_buf, g)
        ratios = []
        for v in range(G * g, G * g + G):
            blurred = z_apply(g_buf[v].reshape(CX * CY, CZ), halo, zf_mat, v)
            ratio = o_buf[v].reshape(CX * CY, CZ) / blurred
            r_buf[v] = ratio.reshape(CX, CY, CZ)
            ratios.append(ratio)
        send_edges(ratios, *backward, g)

    def backward_x(outputs, v, carry):
        t = x_taps(v)
        for xo in outputs:
            accs = []
            for h in range(CY // 8):
                ys = pl.ds(8 * h, 8)
                acc = None
                for xi in range(max(0, xo - T + 1), min(CX, xo + 1)):
                    term = t[xo - xi] * g_buf[v, xi, ys, :]
                    acc = term if acc is None else acc + term
                accs.append(acc)
            hi, lo = split(jnp.concatenate(accs, axis=0))
            x_buf[v, xo, 0:CY, :] = hi
            x_buf[v, xo, CY:2 * CY, :] = lo
        return carry

    for g in range(V // G):
        finish((part(z_copy, *backward, g),), "bz")
        halo = halo_rows(hb_buf, g)
        for v in range(G * g, G * g + G):
            f = r_buf[v].reshape(CX * CY, CZ)
            g_buf[v] = z_apply(f, halo, zb_mat, v).reshape(CX, CY, CZ)
        lax.fori_loop(G * g, G * g + G, part(backward_x, halo_planes), 0)

    def backward_y(x0, xb):
        full = None
        for v in range(V):
            data = []
            for h in range(2):
                planes = x_buf[v, x0 + 4 * h:x0 + 4 * h + 4].reshape(128, CZ)
                data.append(jnp.concatenate([planes, planes], axis=0))
            term = dot(yb_mat[xb, v], jnp.concatenate(data, axis=1))
            full = term if full is None else full + term
        for h in range(2):
            p_buf[x0 + 4 * h:x0 + 4 * h + 4] = full[:, h * CZ:(h + 1) * CZ].reshape(4, EY, CZ)

    backward_y(0, 0)
    backward_y(EX - 8, 2)
    rx_edges = (part(rx_copy, 1), part(rx_copy, 2))
    rx_own = (part(rx_copy, 0),)
    start(rx_edges + rx_own, "bx")
    lax.fori_loop(0, V, part(backward_x, range(R, R + CX)), 0)
    backward_y(R, 1)
    backward_y(2 * R, 1)

    total = jnp.zeros((8, CZ), F32)
    for xb, xs in ((0, range(0, R)), (1, range(R, R + CX)), (2, range(R + CX, EX))):
        for yb, ys in ((0, (0,)), (1, (1, 2)), (2, (3,))):
            count = jnp.maximum(jnp.sum(w_buf[xb, yb], axis=0, keepdims=True), 1.0)
            term = jnp.zeros((8, CZ), F32)
            for x in xs:
                for t in ys:
                    term = term + e_buf[x, 8 * t:8 * t + 8, :] * p_buf[x, 8 * t:8 * t + 8, :]
            total = total + term / count
    red_own[0] = jnp.where(
        row8 == 0, jnp.sum(red_own[1], axis=0, keepdims=True),
        jnp.where(row8 == 1, jnp.sum(total, axis=0, keepdims=True), 0.0),
    )

    def red_copy(stage, d):
        name, n = LINES[stage]
        return pltpu.make_async_remote_copy(
            src_ref=red_own.at[0 if stage == 0 else stage + 1], dst_ref=red_in.at[stage, d],
            send_sem=red_send.at[stage, d], recv_sem=red_recv.at[stage, d],
            device_id={name: lax.rem(ids[name] + d, n)}, device_id_type=MESH,
        )

    def red_start(stage):
        for d in range(1, LINES[stage][1]):
            red_copy(stage, d).start()

    def red_finish(stage):
        total = red_own[0 if stage == 0 else stage + 1]
        for d in range(1, LINES[stage][1]):
            red_copy(stage, d).wait()
            total = total + red_in[stage, d]
        red_own[stage + 2] = total

    red_start(0)
    red_finish(0)
    red_start(1)

    finish(rx_edges, "bx")
    for t in (0, 3):
        ys = slice(8 * t, 8 * t + 8)
        p_buf[R:2 * R, ys] = p_buf[R:2 * R, ys] + rx_buf[0, :, ys]
        p_buf[2 * R:3 * R, ys] = p_buf[2 * R:3 * R, ys] + rx_buf[1, :, ys]
    start((ry_copy,), "by")
    red_finish(1)
    red_start(2)
    red_finish(2)
    final = red_own[4]
    scale = jnp.sum(final[0:1], axis=1, keepdims=True) / (
        jnp.sum(final[1:2], axis=1, keepdims=True) * count_own[:, 0:1]
    )
    finish(rx_own, "bx")
    finish((ry_copy,), "by")
    for s in range(2):
        xs = slice(R + 8 * s, R + 8 * s + 8)
        for h in range(2):
            ys = slice(R + 8 * h, R + 8 * h + 8)
            summed = p_buf[xs, ys, :] + rx_buf[s, :, ys] + ry_buf[h, 8 * s:8 * s + 8]
            out[8 * s:8 * s + 8, 8 * h:8 * h + 8, :] = e_buf[xs, ys, :] * summed * scale.reshape(1, 1, 1)


def on_device(estimate, observed, coverage, psf_taps):
    dma = pltpu.SemaphoreType.DMA
    arrays = (estimate, observed, coverage.reshape(1, V), jnp.transpose(psf_taps, (1, 0, 2)))
    return pl.pallas_call(
        kernel,
        out_shape=jax.ShapeDtypeStruct((CX, CY, CZ), F32),
        in_specs=[pl.BlockSpec(memory_space=pltpu.HBM)] * 4,
        out_specs=pl.BlockSpec(memory_space=pltpu.VMEM),
        scratch_shapes=[
            pltpu.VMEM((EX, EY, CZ), F32),
            pltpu.VMEM((V, CX, CY, CZ), F32),
            pltpu.VMEM((V, EX, CY, CZ), F32),
            pltpu.VMEM((V, CX, CY, CZ), F32),
            pltpu.VMEM((V, CX, CY, CZ), F32),
            pltpu.VMEM((V, EX, 2 * CY, CZ), BF16),
            pltpu.VMEM((EX, EY, CZ), F32),
            pltpu.VMEM((2, R, EY, CZ), F32),
            pltpu.VMEM((2, CX, R, CZ), F32),
            pltpu.VMEM((V, 2 * R, CX * CY), F32),
            pltpu.VMEM((V, 2 * R, CX * CY), F32),
            pltpu.VMEM((V, 2 * R, CX * CY), F32),
            pltpu.VMEM((V, 2 * R, CX * CY), F32),
            pltpu.VMEM((3, 3, V, CZ), F32),
            pltpu.VMEM((1, V), jnp.int32),
            pltpu.VMEM((3, V, T), F32),
            pltpu.VMEM((3 + T, V, CZ), F32),
            pltpu.VMEM((V, 192, 256), BF16),
            pltpu.VMEM((V, 192, 256), BF16),
            pltpu.VMEM((V, 2 * CY, 256), BF16),
            pltpu.VMEM((3, V, 128, 256), BF16),
            pltpu.VMEM((5, 8, CZ), F32),
            pltpu.VMEM((3, 8, 8, CZ), F32),
            dma((4,)), dma((2,)), dma((2,)), dma((3, 2)), dma((3, 2)), dma((2, 2)), dma((2, 2)),
            dma((2, 2)), dma((2, 2)), dma((2, 2)), dma((2, 2)), dma((3, 2)), dma((3, 2)), dma((2,)), dma((2,)),
            dma((3, 8)), dma((3, 8)),
        ],
        compiler_params=pltpu.CompilerParams(
            collective_id=0, has_side_effects=True, vmem_limit_bytes=48 * 1024 * 1024
        ),
    )(*[pltpu.with_memory_space_constraint(a, pltpu.HBM) for a in arrays])


def solution(mesh):
    block = P("bx", "by", "bz")
    views = P(None, "bx", "by", "bz")
    return jax.shard_map(
        on_device, mesh=mesh, in_specs=(block, views, views, P()), out_specs=block, check_vma=False
    )
```

time: 50.8 us -> 38.3 us (0.75)
  Pallas kernels: 46.4 us -> 37.5 us
  local copies, waits for them, and re-layouts: 4.23 us -> 0.66 us
    pallas_call x1, Pallas kernels: 46.4 us -> 37.5 us  [on_device(): pl.pallas_call(kernel, out_shape=jax.ShapeDtypeStruct((CX, CY, CZ), F32),...]
    unnamed x7 -> x1, local copies, waits for them, and re-layouts: 4.23 us -> 0.66 us
where the time goes in v1:
time: 38.3 us; the launch traced here: 38.2 us
  Pallas kernels  37.5 us (98%)
  local copies, waits for them, and re-layouts  0.66 us (2%)
    pallas_call x1, Pallas kernels, on_device(): pl.pallas_call(kernel, out_shape=jax.ShapeDtypeStruct((CX, CY, CZ), F32),...  37.5 us

profile of v1, /device:TPU:1, one launch (start us, length us, event | category | flops | bytes accessed | tf_op | source)
XLA Modules:
  0.0 38.2 jit_solution(10652039087051681780)
XLA Ops:
  0.0 37.5 %shard_map.46 = f32[16,16,128]{2,1,0:T(8,128)S(1)} custom-call(f32[16,16,128]{2,1,0:T(8,128)} %est.1, f32[8,16,16,128]{3,2,1,0:T(8,128)} %obs.1, s32[1,8]{1,0:T(1,128)} %bitcast.3, f32[3,8,17]{2,1,0:T(8,128)} %bitcast.2), custom_call_target="tpu_custom_call" | custom-call | tf_op jit(solution)/shard_map/pallas_call | solution.py:415
  37.5 0.7 %copy.6 = f32[16,16,128]{2,1,0:T(8,128)} copy(f32[16,16,128]{2,1,0:T(8,128)S(1)} %shard_map.46) | data formatting | bytes 262144

commit v2 on v1

--- a/solution.py
+++ b/solution.py
@@ -15,6 +15,7 @@
 EX, EY = CX + 2 * R, CY + 2 * R
 G = 4
 LINES = (("bz", 4), ("by", 8), ("bx", 4))
+STAGES = (8, 16)
 
 
 def split(f):
@@ -36,10 +37,10 @@
     est, obs, cov, taps, out,
     e_buf, o_buf, y_buf, g_buf, r_buf, x_buf, p_buf, rx_buf, ry_buf,
     sf_buf, hf_buf, sb_buf, hb_buf, w_buf, c_buf, k_buf, t_buf,
-    zf_mat, zb_mat, yf_mat, yb_mat, red_own, red_in,
+    zf_mat, zb_mat, yf_mat, yw_mat, yb_mat, b_buf, seen_buf, red_own, red_in,
     load_sem, y_send, y_recv, x_send, x_recv, w_send, w_recv,
     zf_send, zf_recv, zb_send, zb_recv, rx_send, rx_recv, ry_send, ry_recv,
-    red_send, red_recv,
+    red_send, red_recv, met_sem,
 ):
     ids = {name: lax.axis_index(name) for name, _ in LINES}
     sizes = dict(LINES)
@@ -130,8 +131,9 @@
             def _():
                 for c in copies:
                     c(1 - side).wait_recv()
-                    c(side).wait_send()
-
+                    sent[name, side].append(c)
+
+    sent = {(name, side): [] for name, _ in LINES for side in (0, 1)}
     part = functools.partial
     x_first = (part(x_copy, 0),)
     x_second = (part(x_copy, 1), part(x_copy, 2), xw_copy)
@@ -163,6 +165,11 @@
     w_buf[1, 1] = jnp.broadcast_to(jnp.sum(picked, axis=1, keepdims=True), (V, CZ))
     load_e.wait()
     pl.semaphore_wait(barrier, sum(n - 1 for _, n in LINES))
+    for name, n in LINES:
+        for d in range(1, n):
+            pl.semaphore_signal(
+                met_sem, inc=1, device_id={name: lax.rem(ids[name] + d, n)}, device_id_type=MESH
+            )
     start((y_copy, yw_copy), "by")
     start(x_first, "bx")
 
@@ -194,11 +201,11 @@
     finish((y_copy, yw_copy), "by")
     start(x_second, "bx")
 
-    def forward_y(x0):
+    def forward_y(x0, source=e_buf, mat=yf_mat):
         data = jnp.concatenate(
-            [stack4(e_buf[pl.ds(x0 + 2 * h, 2)].reshape(2 * EY, CZ)) for h in range(2)], axis=1
-        )
-        full = dot(yf_mat[...].reshape(V * 2 * CY, 256), data)
+            [stack4(source[pl.ds(x0 + 2 * h, 2)].reshape(2 * EY, CZ)) for h in range(2)], axis=1
+        )
+        full = dot(mat[...].reshape(V * 2 * CY, 256), data)
         for h in range(2):
             y_buf[:, pl.ds(x0 + 2 * h, 2)] = full[:, h * CZ:(h + 1) * CZ].reshape(V, 2, CY, CZ)
 
@@ -208,7 +215,7 @@
     def x_taps(v):
         return [jnp.broadcast_to(t_buf[3 + k, pl.ds(v, 1), :], (8, CZ)) for k in range(T)]
 
-    def forward_x(inputs, first, v, carry):
+    def forward_x(inputs, first, g_buf, v, carry):
         t = x_taps(v)
         for h in range(CY // 8):
             ys = pl.ds(8 * h, 8)
@@ -222,7 +229,7 @@
                 g_buf[v, xo, ys, :] = acc[xo]
         return carry
 
-    lax.fori_loop(0, V, part(forward_x, range(R, R + CX), True), 0)
+    lax.fori_loop(0, V, part(forward_x, range(R, R + CX), True, g_buf), 0)
 
     lane = lax.broadcasted_iota(jnp.int32, (128, 128), 1)
     row = lax.broadcasted_iota(jnp.int32, (128, 128), 0)
@@ -249,7 +256,7 @@
     for v in range(V):
         seen = seen + w_buf[1, 1, v:v + 1, :] * jnp.sum(o_buf[v].reshape(CX * CY // 8, 8, CZ), axis=0)
     count_own = jnp.sum(w_buf[1, 1], axis=0, keepdims=True)
-    red_own[1] = seen / count_own
+    seen_buf[...] = seen / count_own
 
     finish(x_first + x_second, "bx")
     for x0 in (0, 4, EX - 8, EX - 4):
@@ -277,7 +284,7 @@
     backward = (sb_buf, hb_buf, zb_send, zb_recv)
     halo_planes = tuple(range(R)) + tuple(range(R + CX, EX))
     for g in range(V // G):
-        lax.fori_loop(G * g, G * g + G, part(forward_x, halo_planes, False), 0)
+        lax.fori_loop(G * g, G * g + G, part(forward_x, halo_planes, False, g_buf), 0)
         send_edges(
             [g_buf[v].reshape(CX * CY, CZ) for v in range(G * g, G * g + G)], *forward, g
         )
@@ -292,6 +299,20 @@
             w = jnp.concatenate(w * 4, axis=0).astype(BF16)
             for i in range(2):
                 yb_mat[xb, v, :, 128 * i:128 * i + 128] = both[i] * w
+
+    third = (band % 32)[:8]
+    for xb, xs in ((0, (0, R)), (1, (R, R + CX)), (2, (R + CX, EX))):
+        for yb, ys in ((0, (0, R)), (1, (R, R + CY)), (2, (R + CY, EY))):
+            count = jnp.maximum(jnp.sum(w_buf[xb, yb], axis=0, keepdims=True), 1.0)
+            p_buf[xs[0]:xs[1], ys[0]:ys[1]] = e_buf[xs[0]:xs[1], ys[0]:ys[1]] * (1.0 / count)
+        w = jnp.where(third < R, w_buf[xb, 0], jnp.where(third < R + CY, w_buf[xb, 1], w_buf[xb, 2]))
+        for v in range(V):
+            wide = jnp.broadcast_to(w[v:v + 1], (2 * CY, CZ)).astype(BF16)
+            for i in range(2):
+                cols = slice(128 * i, 128 * i + 128)
+                yw_mat[xb, v, :, cols] = yf_mat[v, :, cols] * wide
+    for x0 in range(0, EX, 4):
+        forward_y(x0, p_buf, yw_mat.at[0 if x0 < R else 1 if x0 < R + CX else 2])
 
     for g in range(V // G):
         finish((part(z_copy, *forward, g),), "bz")
@@ -320,13 +341,66 @@
             x_buf[v, xo, CY:2 * CY, :] = lo
         return carry
 
+    lax.fori_loop(0, V, part(forward_x, range(EX), True, b_buf), 0)
+
+    total = jnp.zeros((8, CZ), F32)
     for g in range(V // G):
         finish((part(z_copy, *backward, g),), "bz")
         halo = halo_rows(hb_buf, g)
         for v in range(G * g, G * g + G):
-            f = r_buf[v].reshape(CX * CY, CZ)
-            g_buf[v] = z_apply(f, halo, zb_mat, v).reshape(CX, CY, CZ)
-        lax.fori_loop(G * g, G * g + G, part(backward_x, halo_planes), 0)
+            f = z_apply(r_buf[v].reshape(CX * CY, CZ), halo, zb_mat, v)
+            g_buf[v] = f.reshape(CX, CY, CZ)
+            weighed = f * b_buf[v].reshape(CX * CY, CZ)
+            total = total + jnp.sum(weighed.reshape(CX * CY // 8, 8, CZ), axis=0)
+
+    lane1 = lax.broadcasted_iota(jnp.int32, (1, CZ), 1)
+
+    def summed(f):
+        return jnp.sum(jnp.sum(f, axis=0, keepdims=True), axis=1, keepdims=True)
+
+    red_own[0] = jnp.where(lane1 < CZ // 2, summed(seen_buf[...]), summed(total))
+
+    by_hi, by_lo = lax.div(ids["by"], 4), lax.rem(ids["by"], 4)
+
+    def red_peer(stage, d):
+        if stage == 0:
+            return {
+                "bx": lax.rem(ids["bx"] + d % 4, 4),
+                "by": lax.rem(by_hi + d // 4, 2) * 4 + by_lo,
+            }
+        return {
+            "bz": lax.rem(ids["bz"] + d % 4, 4),
+            "by": by_hi * 4 + lax.rem(by_lo + d // 4, 4),
+        }
+
+    def red_copy(stage, d):
+        return pltpu.make_async_remote_copy(
+            src_ref=red_own.at[stage], dst_ref=red_in.at[stage, d],
+            send_sem=red_send.at[stage], recv_sem=red_recv.at[stage],
+            device_id=red_peer(stage, d), device_id_type=MESH,
+        )
+
+    def red_start(stage):
+        for d in range(1, STAGES[stage]):
+            red_copy(stage, d).start()
+
+    def red_all(stage):
+        every = red_in.at[stage, pl.ds(1, STAGES[stage] - 1)]
+        return pltpu.make_async_remote_copy(
+            src_ref=every, dst_ref=every, send_sem=red_send.at[stage],
+            recv_sem=red_recv.at[stage], device_id=red_peer(stage, 1), device_id_type=MESH,
+        )
+
+    def red_finish(stage):
+        red_all(stage).wait_recv()
+        total = red_own[stage]
+        for d in range(1, STAGES[stage]):
+            total = total + red_in[stage, d]
+        return total
+
+    pl.semaphore_wait(met_sem, sum(n - 1 for _, n in LINES))
+    red_start(0)
+    lax.fori_loop(0, V, part(backward_x, halo_planes), 0)
 
     def backward_y(x0, xb):
         full = None
@@ -346,45 +420,10 @@
     rx_own = (part(rx_copy, 0),)
     start(rx_edges + rx_own, "bx")
     lax.fori_loop(0, V, part(backward_x, range(R, R + CX)), 0)
+    red_own[1] = red_finish(0)
+    red_start(1)
     backward_y(R, 1)
     backward_y(2 * R, 1)
-
-    total = jnp.zeros((8, CZ), F32)
-    for xb, xs in ((0, range(0, R)), (1, range(R, R + CX)), (2, range(R + CX, EX))):
-        for yb, ys in ((0, (0,)), (1, (1, 2)), (2, (3,))):
-            count = jnp.maximum(jnp.sum(w_buf[xb, yb], axis=0, keepdims=True), 1.0)
-            term = jnp.zeros((8, CZ), F32)
-            for x in xs:
-                for t in ys:
-                    term = term + e_buf[x, 8 * t:8 * t + 8, :] * p_buf[x, 8 * t:8 * t + 8, :]
-            total = total + term / count
-    red_own[0] = jnp.where(
-        row8 == 0, jnp.sum(red_own[1], axis=0, keepdims=True),
-        jnp.where(row8 == 1, jnp.sum(total, axis=0, keepdims=True), 0.0),
-    )
-
-    def red_copy(stage, d):
-        name, n = LINES[stage]
-        return pltpu.make_async_remote_copy(
-            src_ref=red_own.at[0 if stage == 0 else stage + 1], dst_ref=red_in.at[stage, d],
-            send_sem=red_send.at[stage, d], recv_sem=red_recv.at[stage, d],
-            device_id={name: lax.rem(ids[name] + d, n)}, device_id_type=MESH,
-        )
-
-    def red_start(stage):
-        for d in range(1, LINES[stage][1]):
-            red_copy(stage, d).start()
-
-    def red_finish(stage):
-        total = red_own[0 if stage == 0 else stage + 1]
-        for d in range(1, LINES[stage][1]):
-            red_copy(stage, d).wait()
-            total = total + red_in[stage, d]
-        red_own[stage + 2] = total
-
-    red_start(0)
-    red_finish(0)
-    red_start(1)
 
     finish(rx_edges, "bx")
     for t in (0, 3):
@@ -392,13 +431,6 @@
         p_buf[R:2 * R, ys] = p_buf[R:2 * R, ys] + rx_buf[0, :, ys]
         p_buf[2 * R:3 * R, ys] = p_buf[2 * R:3 * R, ys] + rx_buf[1, :, ys]
     start((ry_copy,), "by")
-    red_finish(1)
-    red_start(2)
-    red_finish(2)
-    final = red_own[4]
-    scale = jnp.sum(final[0:1], axis=1, keepdims=True) / (
-        jnp.sum(final[1:2], axis=1, keepdims=True) * count_own[:, 0:1]
-    )
     finish(rx_own, "bx")
     finish((ry_copy,), "by")
     for s in range(2):
@@ -406,7 +438,18 @@
         for h in range(2):
             ys = slice(R + 8 * h, R + 8 * h + 8)
             summed = p_buf[xs, ys, :] + rx_buf[s, :, ys] + ry_buf[h, 8 * s:8 * s + 8]
-            out[8 * s:8 * s + 8, 8 * h:8 * h + 8, :] = e_buf[xs, ys, :] * summed * scale.reshape(1, 1, 1)
+            out[8 * s:8 * s + 8, 8 * h:8 * h + 8, :] = e_buf[xs, ys, :] * summed
+    for name, _ in LINES:
+        for side in (0, 1):
+            @pl.when(has(name, side))
+            def _():
+                for c in sent[name, side]:
+                    c(side).wait_send()
+    red_all(0).wait_send()
+    red_all(1).wait_send()
+    final = red_finish(1)
+    scale = final[:, 0:1] / (final[:, CZ // 2:CZ // 2 + 1] * count_own[:, 0:1])
+    out[...] = out[...] * scale.reshape(1, 1, 1)
 
 
 def on_device(estimate, observed, coverage, psf_taps):
@@ -438,12 +481,15 @@
             pltpu.VMEM((V, 192, 256), BF16),
             pltpu.VMEM((V, 192, 256), BF16),
             pltpu.VMEM((V, 2 * CY, 256), BF16),
+            pltpu.VMEM((3, V, 2 * CY, 256), BF16),
             pltpu.VMEM((3, V, 128, 256), BF16),
-            pltpu.VMEM((5, 8, CZ), F32),
-            pltpu.VMEM((3, 8, 8, CZ), F32),
+            pltpu.VMEM((V, CX, CY, CZ), F32),
+            pltpu.VMEM((8, CZ), F32),
+            pltpu.VMEM((2, 1, CZ), F32),
+            pltpu.VMEM((2, 16, 1, CZ), F32),
             dma((4,)), dma((2,)), dma((2,)), dma((3, 2)), dma((3, 2)), dma((2, 2)), dma((2, 2)),
             dma((2, 2)), dma((2, 2)), dma((2, 2)), dma((2, 2)), dma((3, 2)), dma((3, 2)), dma((2,)), dma((2,)),
-            dma((3, 8)), dma((3, 8)),
+            dma((2,)), dma((2,)), pltpu.SemaphoreType.REGULAR,
         ],
         compiler_params=pltpu.CompilerParams(
             collective_id=0, has_side_effects=True, vmem_limit_bytes=48 * 1024 * 1024

time: 38.3 us -> 31.7 us (0.83)
  Pallas kernels: 37.5 us -> 30.7 us
    pallas_call x1, Pallas kernels: 37.5 us -> 30.7 us  [on_device(): pl.pallas_call(kernel, out_shape=jax.ShapeDtypeStruct((CX, CY, CZ), F32),...]
where the time goes in v2:
time: 31.7 us; the launch traced here: 31.3 us
  Pallas kernels  30.7 us (97%)
  local copies, waits for them, and re-layouts  0.66 us (2%)
    pallas_call x1, Pallas kernels, on_device(): pl.pallas_call(kernel, out_shape=jax.ShapeDtypeStruct((CX, CY, CZ), F32),...  30.7 us
    unnamed x1, local copies, waits for them, and re-layouts  0.66 us

profile of v2, /device:TPU:1, one launch (start us, length us, event | category | flops | bytes accessed | tf_op | source)
XLA Modules:
  0.0 31.3 jit_solution(17509952525348725709)
XLA Ops:
  0.0 30.7 %shard_map.46 = f32[16,16,128]{2,1,0:T(8,128)S(1)} custom-call(f32[16,16,128]{2,1,0:T(8,128)} %est.1, f32[8,16,16,128]{3,2,1,0:T(8,128)} %obs.1, s32[1,8]{1,0:T(1,128)} %bitcast.3, f32[3,8,17]{2,1,0:T(8,128)} %bitcast.2), custom_call_target="tpu_custom_call" | custom-call | tf_op jit(solution)/shard_map/pallas_call | solution.py:458
  30.7 0.7 %copy.6 = f32[16,16,128]{2,1,0:T(8,128)} copy(f32[16,16,128]{2,1,0:T(8,128)S(1)} %shard_map.46) | data formatting | bytes 262144

commit v3 on v2

v3 whole, which is shorter than its diff:
```python
import functools

import jax
import jax.numpy as jnp
from jax import lax
from jax.experimental import pallas as pl
from jax.experimental.pallas import tpu as pltpu
from jax.sharding import PartitionSpec as P

MESH = pl.DeviceIdType.MESH
F32 = jnp.float32
BF16 = jnp.bfloat16
V, R, T = 8, 8, 17
CX, CY, CZ = 16, 16, 128
EX, EY = CX + 2 * R, CY + 2 * R
G = 4
LINES = (("bz", 4), ("by", 8), ("bx", 4))
STAGES = (8, 16)
SIDES = tuple((x, y) for x in (-1, 0, 1) for y in (-1, 0, 1) if x or y)
ROUNDS = (
    (("bz", 1), ("by", 1), ("bx", 1)),
    (("bz", 1), ("by", 1), ("bx", 1)),
    (("bz", 2), ("by", 2), ("bx", 2)),
    (("bz", 2), ("by", 4), ("bx", 2)),
)


def split(f):
    hi = f.astype(BF16)
    lo = (f - hi.astype(F32)).astype(BF16)
    return hi, lo


def dot(a, b):
    return jnp.dot(a, b, preferred_element_type=F32)


def stack4(f):
    hi, lo = split(f)
    return jnp.concatenate([hi, lo, hi, lo], axis=0)


def kernel(
    est, obs, cov, taps, out,
    e_buf, o_buf, y_buf, m_buf, g_buf, r_buf, x_buf, p_buf, rp_buf,
    zt_buf, h_buf, ht_buf, sb_buf, hb_buf, c_buf, k_buf, t_buf, l_buf,
    zf_mat, zb_mat, yf_mat, yw_mat, yb_mat, b_buf, seen_buf, red_own, red_in,
    load_sem, e_send, e_recv, f_send, f_recv, h_send, h_recv,
    zb_send, zb_recv, p_send, p_recv, red_send, red_recv, met_sem,
):
    ids = {name: lax.axis_index(name) for name, _ in LINES}
    sizes = dict(LINES)

    def at(dx, dy, dz=0):
        return {
            name: lax.rem(ids[name] + d + sizes[name], sizes[name])
            for name, d in (("bx", dx), ("by", dy), ("bz", dz)) if d
        }

    barrier = pltpu.get_barrier_semaphore()

    def has(name, d):
        return ids[name] + d >= 0 if d < 0 else ids[name] + d < sizes[name]

    def meet(sem, steps):
        for name, size in steps:
            for d in (-size, size):
                @pl.when(has(name, d))
                def _():
                    pl.semaphore_signal(
                        sem, inc=1, device_id={name: ids[name] + d}, device_id_type=MESH
                    )

    def met(sem, steps):
        heard = 0
        for name, size in steps:
            for d in (-size, size):
                heard = heard + jnp.where(has(name, d), 1, 0)
        pl.semaphore_wait(sem, heard)

    meet(barrier, ROUNDS[0])
    load_e = pltpu.make_async_copy(est, e_buf.at[pl.ds(R, CX), pl.ds(R, CY)], load_sem.at[0])
    load_c = pltpu.make_async_copy(cov, c_buf, load_sem.at[1])
    load_t = pltpu.make_async_copy(taps, k_buf, load_sem.at[2])
    load_o = pltpu.make_async_copy(obs, o_buf, load_sem.at[3])
    for load in (load_e, load_c, load_t, load_o):
        load.start()

    def both(dx, dy):
        if dx and dy:
            return jnp.logical_and(has("bx", dx), has("by", dy))
        return has("bx", dx) if dx else has("by", dy)

    def remote(src, dst, send, recv, device):
        return pltpu.make_async_remote_copy(
            src_ref=src, dst_ref=dst, send_sem=send, recv_sem=recv,
            device_id=device, device_id_type=MESH,
        )

    own = pl.ds(R, CX)
    edge = {-1: pl.ds(0, R), 0: own, 1: pl.ds(EX - R, R)}
    inner = {-1: pl.ds(R, R), 0: own, 1: pl.ds(CX, R)}

    def slot(dx, dy):
        return 3 * (dx + 1) + dy + 1

    def e_copy(dx, dy):
        return remote(
            e_buf.at[inner[dx], inner[dy]], e_buf.at[edge[-dx], edge[-dy]],
            e_send.at[slot(dx, dy)], e_recv.at[slot(-dx, -dy)], at(dx, dy),
        )

    def p_copy(dx, dy):
        return remote(
            p_buf.at[edge[dx], edge[dy]], rp_buf.at[edge[-dx], edge[-dy]],
            p_send.at[slot(dx, dy)], p_recv.at[slot(-dx, -dy)], at(dx, dy),
        )

    rows = {-1: pl.ds(R, R), 1: pl.ds(0, R)}

    def face_copy(dz):
        return remote(
            zt_buf.at[:, rows[dz]], h_buf.at[pl.ds(1, 2), 1, rows[-dz]],
            f_send.at[(1 + dz) // 2], f_recv.at[(1 - dz) // 2], at(0, 0, dz),
        )

    def h_copy(dx, dy):
        src = {-1: pl.ds(1, 1), 0: pl.ds(1, 2), 1: pl.ds(2, 1)}[dx]
        dst = {-1: pl.ds(3, 1), 0: pl.ds(1, 2), 1: pl.ds(0, 1)}[dx]
        return remote(
            h_buf.at[src, 1], h_buf.at[dst, 1 - dy],
            h_send.at[slot(dx, dy)], h_recv.at[slot(-dx, -dy)], at(dx, dy),
        )

    def weight(xb, yb):
        return h_buf[(0, 1, 3)[xb], yb, 2 * R:]

    def z_copy(g, dz):
        views = pl.ds(G * g, G)
        side = (dz + 1) // 2
        return remote(
            sb_buf.at[views, rows[dz]], hb_buf.at[views, rows[-dz]],
            zb_send.at[g, side], zb_recv.at[g, 1 - side], at(0, 0, dz),
        )

    part = functools.partial

    for d in (-1, 1):
        @pl.when(jnp.logical_not(has("by", d)))
        def _():
            e_buf[:, edge[d], :] = jnp.zeros((EX, R, CZ), F32)
            rp_buf[:, edge[d], :] = jnp.zeros((EX, R, CZ), F32)
            h_buf[:, 1 + d] = jnp.zeros((4, 3 * R, CZ), F32)

        @pl.when(jnp.logical_not(has("bx", d)))
        def _():
            e_buf[edge[d]] = jnp.zeros((R, EY, CZ), F32)
            rp_buf[edge[d]] = jnp.zeros((R, EY, CZ), F32)
            h_buf[3 * (1 + d) // 2] = jnp.zeros((3, 3 * R, CZ), F32)

        @pl.when(jnp.logical_not(has("bz", d)))
        def _():
            hb_buf[:, rows[d], :] = jnp.zeros((V, R, CX * CY), F32)
            h_buf[1:3, 1, rows[d], :] = jnp.zeros((2, R, CZ), F32)

    row8 = lax.broadcasted_iota(jnp.int32, (V, CZ), 0)
    lane8 = lax.broadcasted_iota(jnp.int32, (V, CZ), 1)
    load_c.wait()
    flags = jnp.broadcast_to(c_buf[...].astype(F32), (V, V))
    picked = jnp.where(row8[:, :V] == lane8[:, :V], flags, 0.0)
    for b in (1, 2):
        h_buf[b, 1, 2 * R:] = jnp.broadcast_to(jnp.sum(picked, axis=1, keepdims=True), (V, CZ))
    load_e.wait()
    planes = e_buf[own, own].reshape(CX * CY, CZ)
    for h in range(2):
        flipped = planes[128 * h:128 * h + 128].T
        zt_buf[h, 0:R] = flipped[CZ - R:]
        zt_buf[h, R:2 * R] = flipped[:R]
    met(barrier, ROUNDS[0])
    meet(met_sem.at[0], ROUNDS[1])
    for d in (-1, 1):
        @pl.when(has("bz", d))
        def _():
            face_copy(d).start()
    for d in (-1, 1):
        @pl.when(has("bx", d))
        def _():
            e_copy(d, 0).start()
    for d in (-1, 1):
        @pl.when(has("by", d))
        def _():
            e_copy(0, d).start()

    load_t.wait()
    t_buf[...] = jnp.zeros_like(t_buf)
    for d in range(3):
        t_buf[d, 0:V, 0:T] = k_buf[d]
    taps_x, taps_y, taps_z = (
        t_buf[d, 0:V] / jnp.sum(t_buf[d, 0:V], axis=1, keepdims=True) for d in range(3)
    )
    for k, table in enumerate((taps_x, taps_y)):
        wide = jnp.concatenate(
            [jnp.broadcast_to(table[v:v + 1], (2 * R, CZ)) for v in range(V)], axis=0
        ).T
        l_buf[k] = wide[:4 * R]
    taps_y = taps_y + pltpu.roll(taps_y, 32, 1)
    taps_y = taps_y + pltpu.roll(taps_y, 64, 1)
    band = lax.broadcasted_iota(jnp.int32, (CY, 128), 1)
    bands = []
    for v in range(V):
        q = pltpu.roll(
            jnp.broadcast_to(taps_y[v:v + 1], (CY, 128)), 0, 1, stride=1, stride_axis=0
        )
        bands.append(q)
        q_hi, q_lo = split(q)
        zero = jnp.zeros_like(q_hi)
        for x in range(2):
            mine = (band // 32) % 2 == x
            yf_mat[v, x * CY:(x + 1) * CY, 0:128] = jnp.where(mine, q_hi, zero)
            yf_mat[v, x * CY:(x + 1) * CY, 128:256] = jnp.where(mine, q_lo, zero)
    for k in range(T):
        t_buf[3 + k, 0:V] = jnp.broadcast_to(taps_x[:, k:k + 1], (V, CZ))
        t_buf[3 + k, V:2 * V] = jnp.broadcast_to(l_buf[0, k:k + 1], (V, CZ))

    lane = lax.broadcasted_iota(jnp.int32, (128, 128), 1)
    row = lax.broadcasted_iota(jnp.int32, (128, 128), 0)
    near = jnp.abs(row - lane) <= R
    zf_mat[:, 128:256, :] = jnp.zeros((V, 128, 256), BF16)
    zb_mat[:, 128:192, :] = jnp.zeros((V, 64, 256), BF16)
    for v in range(V):
        ring = pltpu.roll(
            jnp.broadcast_to(taps_z[v:v + 1], (128, 128)), 128 - R, 1, stride=1, stride_axis=0
        )
        for mat, full in ((zb_mat, ring), (zf_mat, ring.T)):
            m_hi, m_lo = split(jnp.where(near, full, 0.0))
            mat[v, 0:128, 0:128] = m_hi
            mat[v, 0:128, 128:256] = m_lo
            far = jnp.where(near, 0.0, full)
            far = jnp.concatenate([far[0:R], far[128 - R:128]], axis=0)
            f_hi, f_lo = split(far)
            top = 128 + 2 * R * (v if mat is zf_mat else v % G)
            mat[v, top:top + 2 * R, 0:128] = f_hi
            mat[v, top:top + 2 * R, 128:256] = f_lo

    load_o.wait()
    seen = jnp.zeros((8, CZ), F32)
    for v in range(V):
        seen = seen + weight(1, 1)[v:v + 1] * jnp.sum(o_buf[v].reshape(CX * CY // 8, 8, CZ), axis=0)
    count_own = jnp.sum(weight(1, 1), axis=0, keepdims=True)
    seen_buf[...] = seen / count_own

    met(met_sem.at[0], ROUNDS[1])
    meet(met_sem.at[1], ROUNDS[2])
    for dx in (-1, 1):
        for dy in (-1, 1):
            @pl.when(both(dx, dy))
            def _():
                e_copy(dx, dy).start()
    for d in (-1, 1):
        @pl.when(has("bz", d))
        def _():
            face_copy(-d).wait_recv()
    for dx, dy in SIDES:
        @pl.when(both(dx, dy))
        def _():
            h_copy(dx, dy).start()
    for d in (-1, 1):
        @pl.when(has("by", d))
        def _():
            e_copy(0, -d).wait_recv()

    def forward_y(x0, source=e_buf, mat=yf_mat, to=y_buf):
        data = jnp.concatenate(
            [stack4(source[pl.ds(x0 + 2 * h, 2)].reshape(2 * EY, CZ)) for h in range(2)], axis=1
        )
        full = dot(mat[...].reshape(V * 2 * CY, 256), data)
        for h in range(2):
            to[0:V, pl.ds(x0 + 2 * h, 2)] = full[:, h * CZ:(h + 1) * CZ].reshape(V, 2, CY, CZ)

    for x0 in range(R, R + CX, 4):
        forward_y(x0)

    def x_taps(v):
        return [jnp.broadcast_to(t_buf[3 + k, pl.ds(v, 1), :], (8, CZ)) for k in range(T)]

    def forward_x(inputs, first, y_buf, g_buf, v, carry):
        t = x_taps(v)
        for h in range(CY // 8):
            ys = pl.ds(8 * h, 8)
            acc = [None if first else g_buf[v, xo, ys, :] for xo in range(CX)]
            for xi in inputs:
                val = y_buf[v, xi, ys, :]
                for xo in range(max(0, xi - T + 1), min(CX, xi + 1)):
                    term = t[xi - xo] * val
                    acc[xo] = term if acc[xo] is None else acc[xo] + term
            for xo in range(CX):
                g_buf[v, xo, ys, :] = acc[xo]
        return carry

    def halo_y(b):
        for yb, rows, ys in ((0, slice(R, CY), slice(0, R)), (1, slice(0, CY), slice(R, R + CY)),
                             (2, slice(0, R), slice(R + CY, EY))):
            tile = jnp.concatenate([h_buf[b, yb, :2 * R]] * V, axis=0).T.reshape(R, CY, CZ)
            ht_buf[R * b:R * b + R, ys] = tile[:, rows]

        t = [jnp.broadcast_to(l_buf[1, k:k + 1, :], (8, CZ)) for k in range(T)]
        for x in range(R * b, R * b + R):
            for h in range(2):
                acc = None
                for k in range(T):
                    term = t[k] * ht_buf[x, 8 * h + k:8 * h + k + 8, :]
                    acc = term if acc is None else acc + term
                y_buf[V, x, 8 * h:8 * h + 8, :] = acc

    third = (band % 32)[:8]
    spans = ((0, R), (R, R + CX), (R + CX, EX))

    def mask(xb):
        xs = slice(*spans[xb])
        for yb in range(3):
            ys = slice(*spans[yb])
            count = jnp.maximum(jnp.sum(weight(xb, yb), axis=0, keepdims=True), 1.0)
            p_buf[xs, ys] = e_buf[xs, ys] * (1.0 / count)
        w = jnp.where(third < R, weight(xb, 0), jnp.where(third < R + CY, weight(xb, 1), weight(xb, 2)))
        for v in range(V):
            wide = jnp.broadcast_to(w[v:v + 1], (2 * CY, CZ)).astype(BF16)
            for i in range(2):
                cols = slice(128 * i, 128 * i + 128)
                yw_mat[xb, v, :, cols] = yf_mat[v, :, cols] * wide

    own_planes = range(R, R + CX)
    lax.fori_loop(0, V, part(forward_x, own_planes, True, y_buf, g_buf), 0)
    met(met_sem.at[1], ROUNDS[2])
    meet(met_sem.at[2], ROUNDS[3])
    for d in (-1, 1):
        @pl.when(has("by", d))
        def _():
            h_copy(0, -d).wait_recv()
    halo_y(1)
    halo_y(2)
    forward_x(own_planes, True, y_buf, g_buf, V, 0)
    mask(1)
    for x0 in range(R, R + CX, 4):
        forward_y(x0, p_buf, yw_mat.at[1], m_buf)
    for dx, dy in SIDES:
        if dx:
            @pl.when(both(dx, dy))
            def _():
                e_copy(-dx, -dy).wait_recv()
                h_copy(-dx, -dy).wait_recv()
    for x0 in (0, 4, EX - 8, EX - 4):
        forward_y(x0)
    halo_y(0)
    halo_y(3)
    halo_planes = tuple(range(R)) + tuple(range(R + CX, EX))
    lax.fori_loop(0, V + 1, part(forward_x, halo_planes, False, y_buf, g_buf), 0)

    def send_edges(fields, g):
        for v, f in zip(range(G * g, G * g + G), fields):
            for h in range(2):
                flipped = f[128 * h:128 * h + 128].T
                sb_buf[v, 0:R, 128 * h:128 * h + 128] = flipped[CZ - R:]
                sb_buf[v, R:2 * R, 128 * h:128 * h + 128] = flipped[:R]
        for d in (-1, 1):
            @pl.when(has("bz", d))
            def _():
                z_copy(g, d).start()

    def halo_rows(g):
        flat = hb_buf[G * g:G * g + G].reshape(G * 2 * R, CX * CY)
        return split(jnp.concatenate([flat[:, :128].T, flat[:, 128:].T], axis=0))

    def z_apply(f, halo, mat, v):
        hi, lo = split(f)
        both = dot(jnp.concatenate([hi, halo[0]], axis=1), mat[v])
        rest = dot(jnp.concatenate([lo, halo[1]], axis=1), mat[v, :, 0:128])
        return both[:, :128] + both[:, 128:] + rest

    halo = split(g_buf[V].reshape(CX * CY, CZ))
    for g in range(V // G):
        ratios = []
        for v in range(G * g, G * g + G):
            blurred = z_apply(g_buf[v].reshape(CX * CY, CZ), halo, zf_mat, v)
            ratio = o_buf[v].reshape(CX * CY, CZ) / blurred
            r_buf[v] = ratio.reshape(CX, CY, CZ)
            ratios.append(ratio)
        send_edges(ratios, g)

    for xb, x0s in ((0, (0, 4)), (2, (EX - 8, EX - 4))):
        mask(xb)
        for x0 in x0s:
            forward_y(x0, p_buf, yw_mat.at[xb], m_buf)
    lax.fori_loop(0, V, part(forward_x, range(EX), True, m_buf, b_buf), 0)

    for v in range(V):
        q4 = jnp.concatenate(
            [jnp.where(band // 32 == i // 2, bands[v], 0.0) for i in range(8)], axis=0
        ).T
        pair = split(q4)
        for xb in range(3):
            w = [jnp.broadcast_to(weight(xb, yb)[v:v + 1], (8, CZ)) for yb in (0, 1, 1, 2)]
            w = jnp.concatenate(w * 4, axis=0).astype(BF16)
            for i in range(2):
                yb_mat[xb, v, :, 128 * i:128 * i + 128] = pair[i] * w

    def backward_x(outputs, v, carry):
        t = x_taps(v)
        for xo in outputs:
            accs = []
            for h in range(CY // 8):
                ys = pl.ds(8 * h, 8)
                acc = None
                for xi in range(max(0, xo - T + 1), min(CX, xo + 1)):
                    term = t[xo - xi] * g_buf[v, xi, ys, :]
                    acc = term if acc is None else acc + term
                accs.append(acc)
            hi, lo = split(jnp.concatenate(accs, axis=0))
            x_buf[v, xo, 0:CY, :] = hi
            x_buf[v, xo, CY:2 * CY, :] = lo
        return carry

    total = jnp.zeros((8, CZ), F32)
    for g in range(V // G):
        for d in (-1, 1):
            @pl.when(has("bz", d))
            def _():
                z_copy(g, -d).wait_recv()
        halo = halo_rows(g)
        for v in range(G * g, G * g + G):
            f = z_apply(r_buf[v].reshape(CX * CY, CZ), halo, zb_mat, v)
            g_buf[v] = f.reshape(CX, CY, CZ)
            weighed = f * b_buf[v].reshape(CX * CY, CZ)
            total = total + jnp.sum(weighed.reshape(CX * CY // 8, 8, CZ), axis=0)

    lane1 = lax.broadcasted_iota(jnp.int32, (1, CZ), 1)

    def summed(f):
        return jnp.sum(jnp.sum(f, axis=0, keepdims=True), axis=1, keepdims=True)

    red_own[0] = jnp.where(lane1 < CZ // 2, summed(seen_buf[...]), summed(total))

    by_hi, by_lo = lax.div(ids["by"], 4), lax.rem(ids["by"], 4)

    def red_peer(stage, d):
        if stage == 0:
            return {
                "bx": lax.rem(ids["bx"] + d % 4, 4),
                "by": lax.rem(by_hi + d // 4, 2) * 4 + by_lo,
            }
        return {
            "bz": lax.rem(ids["bz"] + d % 4, 4),
            "by": by_hi * 4 + lax.rem(by_lo + d // 4, 4),
        }

    def red_copy(stage, d):
        return pltpu.make_async_remote_copy(
            src_ref=red_own.at[stage], dst_ref=red_in.at[stage, d],
            send_sem=red_send.at[stage], recv_sem=red_recv.at[stage],
            device_id=red_peer(stage, d), device_id_type=MESH,
        )

    def red_start(stage):
        for d in range(1, STAGES[stage]):
            red_copy(stage, d).start()

    def red_all(stage):
        every = red_in.at[stage, pl.ds(1, STAGES[stage] - 1)]
        return pltpu.make_async_remote_copy(
            src_ref=every, dst_ref=every, send_sem=red_send.at[stage],
            recv_sem=red_recv.at[stage], device_id=red_peer(stage, 1), device_id_type=MESH,
        )

    def red_finish(stage):
        red_all(stage).wait_recv()
        total = red_own[stage]
        for d in range(1, STAGES[stage]):
            total = total + red_in[stage, d]
        return total

    met(met_sem.at[2], ROUNDS[3])
    red_start(0)
    lax.fori_loop(0, V, part(backward_x, halo_planes), 0)

    def backward_y(x0, xb):
        full = None
        for v in range(V):
            data = []
            for h in range(2):
                planes = x_buf[v, x0 + 4 * h:x0 + 4 * h + 4].reshape(128, CZ)
                data.append(jnp.concatenate([planes, planes], axis=0))
            term = dot(yb_mat[xb, v], jnp.concatenate(data, axis=1))
            full = term if full is None else full + term
        for h in range(2):
            p_buf[x0 + 4 * h:x0 + 4 * h + 4] = full[:, h * CZ:(h + 1) * CZ].reshape(4, EY, CZ)

    backward_y(0, 0)
    backward_y(EX - 8, 2)
    for dx in (-1, 1):
        @pl.when(has("bx", dx))
        def _():
            p_copy(dx, 0).start()
        for dy in (-1, 1):
            @pl.when(both(dx, dy))
            def _():
                p_copy(dx, dy).start()
    lax.fori_loop(0, V, part(backward_x, range(R, R + CX)), 0)
    backward_y(R, 1)
    backward_y(2 * R, 1)
    for d in (-1, 1):
        @pl.when(has("by", d))
        def _():
            p_copy(0, d).start()
    red_own[1] = red_finish(0)
    red_start(1)
    for dx, dy in SIDES:
        @pl.when(both(dx, dy))
        def _():
            p_copy(-dx, -dy).wait_recv()
    for s in range(2):
        xs, xe = slice(R + 8 * s, R + 8 * s + 8), edge[2 * s - 1]
        for h in range(2):
            ys, ye = slice(R + 8 * h, R + 8 * h + 8), edge[2 * h - 1]
            summed = p_buf[xs, ys] + rp_buf[xe, ys] + rp_buf[xs, ye] + rp_buf[xe, ye]
            out[8 * s:8 * s + 8, 8 * h:8 * h + 8, :] = e_buf[xs, ys, :] * summed
    for dx, dy in SIDES:
        @pl.when(both(dx, dy))
        def _():
            e_copy(dx, dy).wait_send()
            p_copy(dx, dy).wait_send()
            h_copy(dx, dy).wait_send()
    for d in (-1, 1):
        @pl.when(has("bz", d))
        def _():
            face_copy(d).wait_send()
            for g in range(V // G):
                z_copy(g, d).wait_send()
    red_all(0).wait_send()
    red_all(1).wait_send()
    final = red_finish(1)
    scale = final[:, 0:1] / (final[:, CZ // 2:CZ // 2 + 1] * count_own[:, 0:1])
    out[...] = out[...] * scale.reshape(1, 1, 1)


def on_device(estimate, observed, coverage, psf_taps):
    dma = pltpu.SemaphoreType.DMA
    arrays = (estimate, observed, coverage.reshape(1, V), jnp.transpose(psf_taps, (1, 0, 2)))
    return pl.pallas_call(
        kernel,
        out_shape=jax.ShapeDtypeStruct((CX, CY, CZ), F32),
        in_specs=[pl.BlockSpec(memory_space=pltpu.HBM)] * 4,
        out_specs=pl.BlockSpec(memory_space=pltpu.VMEM),
        scratch_shapes=[
            pltpu.VMEM((EX, EY, CZ), F32),
            pltpu.VMEM((V, CX, CY, CZ), F32),
            pltpu.VMEM((V + 1, EX, CY, CZ), F32),
            pltpu.VMEM((V, EX, CY, CZ), F32),
            pltpu.VMEM((V + 1, CX, CY, CZ), F32),
            pltpu.VMEM((V, CX, CY, CZ), F32),
            pltpu.VMEM((V, EX, 2 * CY, CZ), BF16),
            pltpu.VMEM((EX, EY, CZ), F32),
            pltpu.VMEM((EX, EY, CZ), F32),
            pltpu.VMEM((2, 2 * R, CZ), F32),
            pltpu.VMEM((4, 3, 3 * R, CZ), F32),
            pltpu.VMEM((EX, EY, CZ), F32),
            pltpu.VMEM((V, 2 * R, CX * CY), F32),
            pltpu.VMEM((V, 2 * R, CX * CY), F32),
            pltpu.VMEM((1, V), jnp.int32),
            pltpu.VMEM((3, V, T), F32),
            pltpu.VMEM((3 + T, 2 * V, CZ), F32),
            pltpu.VMEM((2, 4 * R, CZ), F32),
            pltpu.VMEM((V, 256, 256), BF16),
            pltpu.VMEM((V, 192, 256), BF16),
            pltpu.VMEM((V, 2 * CY, 256), BF16),
            pltpu.VMEM((3, V, 2 * CY, 256), BF16),
            pltpu.VMEM((3, V, 128, 256), BF16),
            pltpu.VMEM((V, CX, CY, CZ), F32),
            pltpu.VMEM((8, CZ), F32),
            pltpu.VMEM((2, 1, CZ), F32),
            pltpu.VMEM((2, 16, 1, CZ), F32),
            dma((4,)), dma((9,)), dma((9,)), dma((2,)), dma((2,)), dma((9,)), dma((9,)),
            dma((2, 2)), dma((2, 2)), dma((9,)), dma((9,)), dma((2,)), dma((2,)),
            pltpu.SemaphoreType.REGULAR((3,)),
        ],
        compiler_params=pltpu.CompilerParams(
            collective_id=0, has_side_effects=True, vmem_limit_bytes=48 * 1024 * 1024
        ),
    )(*[pltpu.with_memory_space_constraint(a, pltpu.HBM) for a in arrays])


def solution(mesh):
    block = P("bx", "by", "bz")
    views = P(None, "bx", "by", "bz")
    return jax.shard_map(
        on_device, mesh=mesh, in_specs=(block, views, views, P()), out_specs=block, check_vma=False
    )
```

time: 31.7 us -> 28.6 us (0.902)
  Pallas kernels: 30.7 us -> 27.7 us
    pallas_call x1, Pallas kernels: 30.7 us -> 27.7 us  [on_device(): pl.pallas_call(kernel, out_shape=jax.ShapeDtypeStruct((CX, CY, CZ), F32),...]
where the time goes in v3:
time: 28.6 us; the launch traced here: 28.3 us
  Pallas kernels  27.7 us (97%)
  local copies, waits for them, and re-layouts  0.66 us (2%)
    pallas_call x1, Pallas kernels, on_device(): pl.pallas_call(kernel, out_shape=jax.ShapeDtypeStruct((CX, CY, CZ), F32),...  27.7 us
    unnamed x1, local copies, waits for them, and re-layouts  0.66 us

profile of v3, /device:TPU:1, one launch (start us, length us, event | category | flops | bytes accessed | tf_op | source)
XLA Modules:
  0.0 28.3 jit_solution(14527396325832100001)
XLA Ops:
  0.0 27.7 %shard_map.46 = f32[16,16,128]{2,1,0:T(8,128)S(1)} custom-call(f32[16,16,128]{2,1,0:T(8,128)} %est.1, f32[8,16,16,128]{3,2,1,0:T(8,128)} %obs.1, s32[1,8]{1,0:T(1,128)} %bitcast.3, f32[3,8,17]{2,1,0:T(8,128)} %bitcast.2), custom_call_target="tpu_custom_call" | custom-call | tf_op jit(solution)/shard_map/pallas_call | solution.py:547
  27.7 0.7 %copy.6 = f32[16,16,128]{2,1,0:T(8,128)} copy(f32[16,16,128]{2,1,0:T(8,128)S(1)} %shard_map.46) | data formatting | bytes 262144

commit v4 on v3

--- a/solution.py
+++ b/solution.py
@@ -42,10 +42,10 @@
 
 def kernel(
     est, obs, cov, taps, out,
-    e_buf, o_buf, y_buf, m_buf, g_buf, r_buf, x_buf, p_buf, rp_buf,
-    zt_buf, h_buf, ht_buf, sb_buf, hb_buf, c_buf, k_buf, t_buf, l_buf,
-    zf_mat, zb_mat, yf_mat, yw_mat, yb_mat, b_buf, seen_buf, red_own, red_in,
-    load_sem, e_send, e_recv, f_send, f_recv, h_send, h_recv,
+    e_buf, o_buf, y_buf, m_buf, g_buf, r_buf, x_buf, p_buf, rp_buf, tp_buf,
+    zt_buf, share_buf, h_buf, ht_buf, sb_buf, hb_buf, w_buf, c_buf, k_buf, t_buf, l_buf,
+    zf_mat, zm_mat, zh_mat, yf_mat, yw_mat, yb_mat, b_buf, seen_buf, red_own, red_in,
+    load_sem, e_send, e_recv, w_send, w_recv, f_send, f_recv, h_send, h_recv,
     zb_send, zb_recv, p_send, p_recv, red_send, red_recv, met_sem,
 ):
     ids = {name: lax.axis_index(name) for name, _ in LINES}
@@ -71,14 +71,31 @@
                         sem, inc=1, device_id={name: ids[name] + d}, device_id_type=MESH
                     )
 
-    def met(sem, steps):
-        heard = 0
+    def met(sem, steps, heard=0):
         for name, size in steps:
             for d in (-size, size):
                 heard = heard + jnp.where(has(name, d), 1, 0)
         pl.semaphore_wait(sem, heard)
 
+    def twin(dx):
+        return lax.rem(ids["bx"], 2) == (1 - dx) // 2
+
+    def cross(dx):
+        return jnp.logical_and(has("bx", dx), jnp.logical_not(twin(dx)))
+
+    def cross_both(dx, dy):
+        return jnp.logical_and(cross(dx), has("by", dy))
+
+    corners = [(dx, dy) for dx in (-1, 1) for dy in (-1, 1)]
     meet(barrier, ROUNDS[0])
+    greeted = 0
+    for dx, dy in corners:
+        near_by = jnp.logical_and(has("bx", dx), has("by", dy))
+        greeted = greeted + jnp.where(near_by, 1, 0)
+
+        @pl.when(near_by)
+        def _():
+            pl.semaphore_signal(barrier, inc=1, device_id=at(dx, dy), device_id_type=MESH)
     load_e = pltpu.make_async_copy(est, e_buf.at[pl.ds(R, CX), pl.ds(R, CY)], load_sem.at[0])
     load_c = pltpu.make_async_copy(cov, c_buf, load_sem.at[1])
     load_t = pltpu.make_async_copy(taps, k_buf, load_sem.at[2])
@@ -101,27 +118,59 @@
     edge = {-1: pl.ds(0, R), 0: own, 1: pl.ds(EX - R, R)}
     inner = {-1: pl.ds(R, R), 0: own, 1: pl.ds(CX, R)}
 
-    def slot(dx, dy):
-        return 3 * (dx + 1) + dy + 1
+    def counted(act):
+        ends = [
+            jnp.logical_and(has(name, -1), has(name, 1)) for name in ("bx", "by")
+        ]
+        for nx in (1, 2):
+            for ny in (1, 2):
+                hit = [e if n == 2 else jnp.logical_not(e) for e, n in zip(ends, (nx, ny))]
+
+                @pl.when(jnp.logical_and(*hit))
+                def _():
+                    act(nx, ny)
+
+    def planes_of(buf, rows):
+        width = 32 if rows % 32 == 0 else 24
+        return buf.at[pl.ds(0, rows // width), pl.ds(0, width)]
+
+    def group(ref, send, recv):
+        return remote(ref, ref, send, recv, at(0, 0, 1))
 
     def e_copy(dx, dy):
         return remote(
             e_buf.at[inner[dx], inner[dy]], e_buf.at[edge[-dx], edge[-dy]],
-            e_send.at[slot(dx, dy)], e_recv.at[slot(-dx, -dy)], at(dx, dy),
+            e_send.at[0], e_recv.at[0 if dx else (3 - dy) // 2], at(dx, dy),
+        )
+
+    def e_pass(dx, dy):
+        return remote(
+            e_buf.at[inner[dx], edge[dy]], e_buf.at[edge[-dx], edge[dy]],
+            e_send.at[0], e_recv.at[0], at(dx, 0),
         )
 
     def p_copy(dx, dy):
         return remote(
             p_buf.at[edge[dx], edge[dy]], rp_buf.at[edge[-dx], edge[-dy]],
-            p_send.at[slot(dx, dy)], p_recv.at[slot(-dx, -dy)], at(dx, dy),
-        )
+            p_send.at[0], p_recv.at[0], at(dx, dy),
+        )
+
+    def p_pass(dx):
+        return remote(p_buf.at[edge[dx]], tp_buf, p_send.at[0], p_recv.at[1], at(dx, 0))
 
     rows = {-1: pl.ds(R, R), 1: pl.ds(0, R)}
+    to_rows = {-1: pl.ds(R, R), 1: pl.ds(0, R)}
 
     def face_copy(dz):
         return remote(
-            zt_buf.at[:, rows[dz]], h_buf.at[pl.ds(1, 2), 1, rows[-dz]],
+            zt_buf.at[:, rows[dz]], h_buf.at[pl.ds(1, 2), 1, to_rows[dz]],
             f_send.at[(1 + dz) // 2], f_recv.at[(1 - dz) // 2], at(0, 0, dz),
+        )
+
+    def share_copy(dz):
+        return remote(
+            share_buf.at[2], share_buf.at[(1 - dz) // 2],
+            f_send.at[2 + (1 + dz) // 2], f_recv.at[2 + (1 - dz) // 2], at(0, 0, dz),
         )
 
     def h_copy(dx, dy):
@@ -129,11 +178,14 @@
         dst = {-1: pl.ds(3, 1), 0: pl.ds(1, 2), 1: pl.ds(0, 1)}[dx]
         return remote(
             h_buf.at[src, 1], h_buf.at[dst, 1 - dy],
-            h_send.at[slot(dx, dy)], h_recv.at[slot(-dx, -dy)], at(dx, dy),
-        )
-
-    def weight(xb, yb):
-        return h_buf[(0, 1, 3)[xb], yb, 2 * R:]
+            h_send.at[0], h_recv.at[1 if dx else 0], at(dx, dy),
+        )
+
+    def w_copy(dx, dy):
+        return remote(
+            w_buf.at[1, 1], w_buf.at[1 - dx, 1 - dy],
+            w_send.at[0], w_recv.at[1 if dx else 0], at(dx, dy),
+        )
 
     def z_copy(g, dz):
         views = pl.ds(G * g, G)
@@ -151,37 +203,49 @@
             e_buf[:, edge[d], :] = jnp.zeros((EX, R, CZ), F32)
             rp_buf[:, edge[d], :] = jnp.zeros((EX, R, CZ), F32)
             h_buf[:, 1 + d] = jnp.zeros((4, 3 * R, CZ), F32)
+            w_buf[:, 1 + d] = jnp.zeros((3, V, CZ), F32)
 
         @pl.when(jnp.logical_not(has("bx", d)))
         def _():
             e_buf[edge[d]] = jnp.zeros((R, EY, CZ), F32)
+            h_buf[3 * (1 + d) // 2] = jnp.zeros((3, 3 * R, CZ), F32)
+            w_buf[1 + d] = jnp.zeros((3, V, CZ), F32)
+
+        @pl.when(jnp.logical_not(cross(d)))
+        def _():
             rp_buf[edge[d]] = jnp.zeros((R, EY, CZ), F32)
-            h_buf[3 * (1 + d) // 2] = jnp.zeros((3, 3 * R, CZ), F32)
 
         @pl.when(jnp.logical_not(has("bz", d)))
         def _():
             hb_buf[:, rows[d], :] = jnp.zeros((V, R, CX * CY), F32)
-            h_buf[1:3, 1, rows[d], :] = jnp.zeros((2, R, CZ), F32)
+            h_buf[1:3, 1, to_rows[-d], :] = jnp.zeros((2, R, CZ), F32)
+            share_buf[(1 + d) // 2] = jnp.zeros((V, CZ), F32)
 
     row8 = lax.broadcasted_iota(jnp.int32, (V, CZ), 0)
     lane8 = lax.broadcasted_iota(jnp.int32, (V, CZ), 1)
     load_c.wait()
     flags = jnp.broadcast_to(c_buf[...].astype(F32), (V, V))
     picked = jnp.where(row8[:, :V] == lane8[:, :V], flags, 0.0)
-    for b in (1, 2):
-        h_buf[b, 1, 2 * R:] = jnp.broadcast_to(jnp.sum(picked, axis=1, keepdims=True), (V, CZ))
+    weight = jnp.broadcast_to(jnp.sum(picked, axis=1, keepdims=True), (V, CZ))
+    w_buf[1, 1] = weight
+    share_buf[2] = weight / jnp.sum(weight, axis=0, keepdims=True)
     load_e.wait()
     planes = e_buf[own, own].reshape(CX * CY, CZ)
     for h in range(2):
         flipped = planes[128 * h:128 * h + 128].T
         zt_buf[h, 0:R] = flipped[CZ - R:]
         zt_buf[h, R:2 * R] = flipped[:R]
-    met(barrier, ROUNDS[0])
+    met(barrier, ROUNDS[0], greeted)
     meet(met_sem.at[0], ROUNDS[1])
     for d in (-1, 1):
         @pl.when(has("bz", d))
         def _():
             face_copy(d).start()
+            share_copy(d).start()
+    for dx, dy in SIDES:
+        @pl.when(both(dx, dy))
+        def _():
+            w_copy(dx, dy).start()
     for d in (-1, 1):
         @pl.when(has("bx", d))
         def _():
@@ -190,6 +254,10 @@
         @pl.when(has("by", d))
         def _():
             e_copy(0, d).start()
+    for dx, dy in corners:
+        @pl.when(cross_both(dx, dy))
+        def _():
+            e_copy(dx, dy).start()
 
     load_t.wait()
     t_buf[...] = jnp.zeros_like(t_buf)
@@ -226,40 +294,50 @@
     row = lax.broadcasted_iota(jnp.int32, (128, 128), 0)
     near = jnp.abs(row - lane) <= R
     zf_mat[:, 128:256, :] = jnp.zeros((V, 128, 256), BF16)
-    zb_mat[:, 128:192, :] = jnp.zeros((V, 64, 256), BF16)
+    zh_mat[...] = jnp.zeros_like(zh_mat)
     for v in range(V):
         ring = pltpu.roll(
             jnp.broadcast_to(taps_z[v:v + 1], (128, 128)), 128 - R, 1, stride=1, stride_axis=0
         )
-        for mat, full in ((zb_mat, ring), (zf_mat, ring.T)):
-            m_hi, m_lo = split(jnp.where(near, full, 0.0))
-            mat[v, 0:128, 0:128] = m_hi
-            mat[v, 0:128, 128:256] = m_lo
-            far = jnp.where(near, 0.0, full)
-            far = jnp.concatenate([far[0:R], far[128 - R:128]], axis=0)
-            f_hi, f_lo = split(far)
-            top = 128 + 2 * R * (v if mat is zf_mat else v % G)
-            mat[v, top:top + 2 * R, 0:128] = f_hi
-            mat[v, top:top + 2 * R, 128:256] = f_lo
+        ahead = ring.T
+        m_hi, m_lo = split(jnp.where(near, ahead, 0.0))
+        zf_mat[v, 0:128, 0:128] = m_hi
+        zf_mat[v, 0:128, 128:256] = m_lo
+        far = jnp.where(near, 0.0, ahead)
+        f_hi, f_lo = split(jnp.concatenate([far[128 - R:128], far[0:R]], axis=0))
+        top = 128 + 2 * R * v
+        zf_mat[v, top:top + 2 * R, 0:128] = f_hi
+        zf_mat[v, top:top + 2 * R, 128:256] = f_lo
+        m_hi, m_lo = split(jnp.where(near, ring, 0.0))
+        far = jnp.where(near, 0.0, ring)
+        s_hi, s_lo = split(pltpu.roll(far, (2 * R * v + R) % 128, 1))
+        for i in range(2):
+            zm_mat[v, 128 * i:128 * i + 128, 0:128] = m_hi
+            zm_mat[v, 128 * i:128 * i + 128, 128:256] = s_hi
+        zm_mat[v, 256:384, 0:128] = m_lo
+        zm_mat[v, 256:384, 128:256] = s_lo
+        f_hi, f_lo = split(jnp.concatenate([far[0:R], far[128 - R:128]], axis=0))
+        top = 2 * R * (v % G)
+        zh_mat[v, top:top + 2 * R] = f_hi
+        zh_mat[v, 64 + top:64 + top + 2 * R] = f_hi
+        zh_mat[v, 128 + top:128 + top + 2 * R] = f_lo
 
     load_o.wait()
     seen = jnp.zeros((8, CZ), F32)
     for v in range(V):
-        seen = seen + weight(1, 1)[v:v + 1] * jnp.sum(o_buf[v].reshape(CX * CY // 8, 8, CZ), axis=0)
-    count_own = jnp.sum(weight(1, 1), axis=0, keepdims=True)
+        seen = seen + w_buf[1, 1, v:v + 1] * jnp.sum(o_buf[v].reshape(CX * CY // 8, 8, CZ), axis=0)
+    count_own = jnp.sum(w_buf[1, 1], axis=0, keepdims=True)
     seen_buf[...] = seen / count_own
 
+    for d in (-1, 1):
+        @pl.when(has("bz", d))
+        def _():
+            face_copy(-d).wait_recv()
+            share_copy(-d).wait_recv()
+    for b in (1, 2):
+        h_buf[b, 1, 2 * R:] = jnp.where(lane8 < CZ // 2, share_buf[0], share_buf[1])
     met(met_sem.at[0], ROUNDS[1])
     meet(met_sem.at[1], ROUNDS[2])
-    for dx in (-1, 1):
-        for dy in (-1, 1):
-            @pl.when(both(dx, dy))
-            def _():
-                e_copy(dx, dy).start()
-    for d in (-1, 1):
-        @pl.when(has("bz", d))
-        def _():
-            face_copy(-d).wait_recv()
     for dx, dy in SIDES:
         @pl.when(both(dx, dy))
         def _():
@@ -268,6 +346,10 @@
         @pl.when(has("by", d))
         def _():
             e_copy(0, -d).wait_recv()
+            for dx in (-1, 1):
+                @pl.when(twin(dx))
+                def _():
+                    e_pass(dx, d).start()
 
     def forward_y(x0, source=e_buf, mat=yf_mat, to=y_buf):
         data = jnp.concatenate(
@@ -297,12 +379,25 @@
                 g_buf[v, xo, ys, :] = acc[xo]
         return carry
 
-    def halo_y(b):
-        for yb, rows, ys in ((0, slice(R, CY), slice(0, R)), (1, slice(0, CY), slice(R, R + CY)),
-                             (2, slice(0, R), slice(R + CY, EY))):
+    y_spans = ((0, slice(R, CY), slice(0, R)), (1, slice(0, CY), slice(R, R + CY)),
+               (2, slice(0, R), slice(R + CY, EY)))
+
+    def halo_in(b):
+        for yb, part_of, ys in y_spans:
             tile = jnp.concatenate([h_buf[b, yb, :2 * R]] * V, axis=0).T.reshape(R, CY, CZ)
-            ht_buf[R * b:R * b + R, ys] = tile[:, rows]
-
+            ht_buf[R * b:R * b + R, ys] = tile[:, part_of]
+
+    def halo_share(b):
+        for yb, _, ys in y_spans:
+            tile = h_buf[b, yb, 2 * R:]
+            before = jnp.broadcast_to(tile[:, 0:1], (V, CZ))
+            after = jnp.broadcast_to(tile[:, CZ // 2:CZ // 2 + 1], (V, CZ))
+            share = jnp.where(lane8 % (2 * R) < R, before, after)
+            share = jnp.sum(jnp.where(lane8 // (2 * R) == row8, share, 0.0), axis=0, keepdims=True)
+            at_x = slice(R * b, R * b + R)
+            ht_buf[at_x, ys] = ht_buf[at_x, ys] * share
+
+    def halo_y(b, to):
         t = [jnp.broadcast_to(l_buf[1, k:k + 1, :], (8, CZ)) for k in range(T)]
         for x in range(R * b, R * b + R):
             for h in range(2):
@@ -310,7 +405,7 @@
                 for k in range(T):
                     term = t[k] * ht_buf[x, 8 * h + k:8 * h + k + 8, :]
                     acc = term if acc is None else acc + term
-                y_buf[V, x, 8 * h:8 * h + 8, :] = acc
+                to[V, x, 8 * h:8 * h + 8, :] = acc
 
     third = (band % 32)[:8]
     spans = ((0, R), (R, R + CX), (R + CX, EX))
@@ -319,9 +414,9 @@
         xs = slice(*spans[xb])
         for yb in range(3):
             ys = slice(*spans[yb])
-            count = jnp.maximum(jnp.sum(weight(xb, yb), axis=0, keepdims=True), 1.0)
+            count = jnp.maximum(jnp.sum(w_buf[xb, yb], axis=0, keepdims=True), 1.0)
             p_buf[xs, ys] = e_buf[xs, ys] * (1.0 / count)
-        w = jnp.where(third < R, weight(xb, 0), jnp.where(third < R + CY, weight(xb, 1), weight(xb, 2)))
+        w = jnp.where(third < R, w_buf[xb, 0], jnp.where(third < R + CY, w_buf[xb, 1], w_buf[xb, 2]))
         for v in range(V):
             wide = jnp.broadcast_to(w[v:v + 1], (2 * CY, CZ)).astype(BF16)
             for i in range(2):
@@ -330,30 +425,46 @@
 
     own_planes = range(R, R + CX)
     lax.fori_loop(0, V, part(forward_x, own_planes, True, y_buf, g_buf), 0)
+    halo_planes = tuple(range(R)) + tuple(range(R + CX, EX))
+
+    def masked_y(xb):
+        mask(xb)
+        for x0 in range(spans[xb][0], spans[xb][1], 4):
+            forward_y(x0, p_buf, yw_mat.at[xb], m_buf)
+
+    def w_arrivals(nx, ny):
+        group(w_buf.at[0, pl.ds(0, ny)], w_send.at[0], w_recv.at[0]).wait_recv()
+
+    counted(w_arrivals)
+    masked_y(1)
+    lax.fori_loop(0, V, part(forward_x, own_planes, True, m_buf, b_buf), 0)
+    def x_arrivals(nx, ny):
+        group(planes_of(e_buf, nx * (128 + 64 * ny)), e_send.at[0], e_recv.at[0]).wait_recv()
+        tiles = w_buf.at[pl.ds(0, nx), pl.ds(0, 3)] if ny == 2 else w_buf.at[pl.ds(0, 2), pl.ds(0, nx)]
+        group(tiles, w_send.at[0], w_recv.at[1]).wait_recv()
+
+    counted(x_arrivals)
+    for x0 in (0, 4, EX - 8, EX - 4):
+        forward_y(x0)
+    lax.fori_loop(0, V, part(forward_x, halo_planes, False, y_buf, g_buf), 0)
+    masked_y(0)
+    masked_y(2)
+    lax.fori_loop(0, V, part(forward_x, halo_planes, False, m_buf, b_buf), 0)
     met(met_sem.at[1], ROUNDS[2])
     meet(met_sem.at[2], ROUNDS[3])
-    for d in (-1, 1):
-        @pl.when(has("by", d))
-        def _():
-            h_copy(0, -d).wait_recv()
-    halo_y(1)
-    halo_y(2)
-    forward_x(own_planes, True, y_buf, g_buf, V, 0)
-    mask(1)
-    for x0 in range(R, R + CX, 4):
-        forward_y(x0, p_buf, yw_mat.at[1], m_buf)
-    for dx, dy in SIDES:
-        if dx:
-            @pl.when(both(dx, dy))
-            def _():
-                e_copy(-dx, -dy).wait_recv()
-                h_copy(-dx, -dy).wait_recv()
-    for x0 in (0, 4, EX - 8, EX - 4):
-        forward_y(x0)
-    halo_y(0)
-    halo_y(3)
-    halo_planes = tuple(range(R)) + tuple(range(R + CX, EX))
-    lax.fori_loop(0, V + 1, part(forward_x, halo_planes, False, y_buf, g_buf), 0)
+
+    def h_arrivals(nx, ny):
+        group(h_buf.at[pl.ds(0, 2 * ny), 0], h_send.at[0], h_recv.at[0]).wait_recv()
+        blocks = {2: pl.ds(0, nx), 1: pl.ds(0, 2 * nx)}[ny]
+        cols = pl.ds(0, 3) if ny == 2 else 0
+        group(h_buf.at[blocks, cols], h_send.at[0], h_recv.at[1]).wait_recv()
+
+    counted(h_arrivals)
+    for b in range(4):
+        halo_in(b)
+    for b in range(4):
+        halo_y(b, y_buf)
+    forward_x(range(EX), True, y_buf, g_buf, V, 0)
 
     def send_edges(fields, g):
         for v, f in zip(range(G * g, G * g + G), fields):
@@ -368,7 +479,10 @@
 
     def halo_rows(g):
         flat = hb_buf[G * g:G * g + G].reshape(G * 2 * R, CX * CY)
-        return split(jnp.concatenate([flat[:, :128].T, flat[:, 128:].T], axis=0))
+        hi = flat.astype(BF16).astype(F32)
+        pair = jnp.concatenate([hi, flat - hi], axis=0)
+        pair = jnp.concatenate([pair[:, :128].T, pair[:, 128:].T], axis=0).astype(BF16)
+        return jnp.concatenate([pair, pair[:, :64]], axis=1)
 
     def z_apply(f, halo, mat, v):
         hi, lo = split(f)
@@ -386,19 +500,76 @@
             ratios.append(ratio)
         send_edges(ratios, g)
 
-    for xb, x0s in ((0, (0, 4)), (2, (EX - 8, EX - 4))):
-        mask(xb)
-        for x0 in x0s:
-            forward_y(x0, p_buf, yw_mat.at[xb], m_buf)
-    lax.fori_loop(0, V, part(forward_x, range(EX), True, m_buf, b_buf), 0)
-
+    total = jnp.zeros((8, CZ), F32)
+    outside = jnp.zeros((CX * CY, CZ), F32)
+    for v in range(V):
+        hi, lo = split(r_buf[v].reshape(CX * CY, CZ))
+        f = dot(jnp.concatenate([hi, lo], axis=1), zm_mat[v, 0:256]) + dot(hi, zm_mat[v, 256:384])
+        g_buf[v] = f[:, :128].reshape(CX, CY, CZ)
+        outside = outside + f[:, 128:]
+        weighed = f[:, :128] * b_buf[v].reshape(CX * CY, CZ)
+        total = total + jnp.sum(weighed.reshape(CX * CY // 8, 8, CZ), axis=0)
+    for b in range(4):
+        halo_share(b)
+    for b in range(4):
+        halo_y(b, m_buf)
+    forward_x(range(EX), True, m_buf, b_buf, V, 0)
+    weighed = outside * b_buf[V].reshape(CX * CY, CZ)
+    total = total + jnp.sum(weighed.reshape(CX * CY // 8, 8, CZ), axis=0)
+    lane1 = lax.broadcasted_iota(jnp.int32, (1, CZ), 1)
+
+    def summed(f):
+        return jnp.sum(jnp.sum(f, axis=0, keepdims=True), axis=1, keepdims=True)
+
+    red_own[0] = jnp.where(lane1 < CZ // 2, summed(seen_buf[...]), summed(total))
+
+    by_hi, by_lo = lax.div(ids["by"], 4), lax.rem(ids["by"], 4)
+
+    def red_peer(stage, d):
+        if stage == 0:
+            return {
+                "bx": lax.rem(ids["bx"] + d % 4, 4),
+                "by": lax.rem(by_hi + d // 4, 2) * 4 + by_lo,
+            }
+        return {
+            "bz": lax.rem(ids["bz"] + d % 4, 4),
+            "by": by_hi * 4 + lax.rem(by_lo + d // 4, 4),
+        }
+
+    def red_copy(stage, d):
+        return pltpu.make_async_remote_copy(
+            src_ref=red_own.at[stage], dst_ref=red_in.at[stage, d],
+            send_sem=red_send.at[stage], recv_sem=red_recv.at[stage],
+            device_id=red_peer(stage, d), device_id_type=MESH,
+        )
+
+    def red_start(stage):
+        for d in range(1, STAGES[stage]):
+            red_copy(stage, d).start()
+
+    def red_all(stage):
+        every = red_in.at[stage, pl.ds(1, STAGES[stage] - 1)]
+        return pltpu.make_async_remote_copy(
+            src_ref=every, dst_ref=every, send_sem=red_send.at[stage],
+            recv_sem=red_recv.at[stage], device_id=red_peer(stage, 1), device_id_type=MESH,
+        )
+
+    def red_finish(stage):
+        red_all(stage).wait_recv()
+        total = red_own[stage]
+        for d in range(1, STAGES[stage]):
+            total = total + red_in[stage, d]
+        return total
+
+    met(met_sem.at[2], ROUNDS[3])
+    red_start(0)
     for v in range(V):
         q4 = jnp.concatenate(
             [jnp.where(band // 32 == i // 2, bands[v], 0.0) for i in range(8)], axis=0
         ).T
         pair = split(q4)
         for xb in range(3):
-            w = [jnp.broadcast_to(weight(xb, yb)[v:v + 1], (8, CZ)) for yb in (0, 1, 1, 2)]
+            w = [jnp.broadcast_to(w_buf[xb, yb, v:v + 1], (8, CZ)) for yb in (0, 1, 1, 2)]
             w = jnp.concatenate(w * 4, axis=0).astype(BF16)
             for i in range(2):
                 yb_mat[xb, v, :, 128 * i:128 * i + 128] = pair[i] * w
@@ -419,7 +590,6 @@
             x_buf[v, xo, CY:2 * CY, :] = lo
         return carry
 
-    total = jnp.zeros((8, CZ), F32)
     for g in range(V // G):
         for d in (-1, 1):
             @pl.when(has("bz", d))
@@ -427,58 +597,8 @@
                 z_copy(g, -d).wait_recv()
         halo = halo_rows(g)
         for v in range(G * g, G * g + G):
-            f = z_apply(r_buf[v].reshape(CX * CY, CZ), halo, zb_mat, v)
-            g_buf[v] = f.reshape(CX, CY, CZ)
-            weighed = f * b_buf[v].reshape(CX * CY, CZ)
-            total = total + jnp.sum(weighed.reshape(CX * CY // 8, 8, CZ), axis=0)
-
-    lane1 = lax.broadcasted_iota(jnp.int32, (1, CZ), 1)
-
-    def summed(f):
-        return jnp.sum(jnp.sum(f, axis=0, keepdims=True), axis=1, keepdims=True)
-
-    red_own[0] = jnp.where(lane1 < CZ // 2, summed(seen_buf[...]), summed(total))
-
-    by_hi, by_lo = lax.div(ids["by"], 4), lax.rem(ids["by"], 4)
-
-    def red_peer(stage, d):
-        if stage == 0:
-            return {
-                "bx": lax.rem(ids["bx"] + d % 4, 4),
-                "by": lax.rem(by_hi + d // 4, 2) * 4 + by_lo,
-            }
-        return {
-            "bz": lax.rem(ids["bz"] + d % 4, 4),
-            "by": by_hi * 4 + lax.rem(by_lo + d // 4, 4),
-        }
-
-    def red_copy(stage, d):
-        return pltpu.make_async_remote_copy(
-            src_ref=red_own.at[stage], dst_ref=red_in.at[stage, d],
-            send_sem=red_send.at[stage], recv_sem=red_recv.at[stage],
-            device_id=red_peer(stage, d), device_id_type=MESH,
-        )
-
-    def red_start(stage):
-        for d in range(1, STAGES[stage]):
-            red_copy(stage, d).start()
-
-    def red_all(stage):
-        every = red_in.at[stage, pl.ds(1, STAGES[stage] - 1)]
-        return pltpu.make_async_remote_copy(
-            src_ref=every, dst_ref=every, send_sem=red_send.at[stage],
-            recv_sem=red_recv.at[stage], device_id=red_peer(stage, 1), device_id_type=MESH,
-        )
-
-    def red_finish(stage):
-        red_all(stage).wait_recv()
-        total = red_own[stage]
-        for d in range(1, STAGES[stage]):
-            total = total + red_in[stage, d]
-        return total
-
-    met(met_sem.at[2], ROUNDS[3])
-    red_start(0)
+            g_buf[v] = g_buf[v] + dot(halo, zh_mat[v]).reshape(CX, CY, CZ)
+
     lax.fori_loop(0, V, part(backward_x, halo_planes), 0)
 
     def backward_y(x0, xb):
@@ -496,42 +616,57 @@
     backward_y(0, 0)
     backward_y(EX - 8, 2)
     for dx in (-1, 1):
-        @pl.when(has("bx", dx))
+        @pl.when(twin(dx))
+        def _():
+            p_pass(dx).start()
+
+        @pl.when(cross(dx))
         def _():
             p_copy(dx, 0).start()
         for dy in (-1, 1):
-            @pl.when(both(dx, dy))
+            @pl.when(cross_both(dx, dy))
             def _():
                 p_copy(dx, dy).start()
     lax.fori_loop(0, V, part(backward_x, range(R, R + CX)), 0)
     backward_y(R, 1)
     backward_y(2 * R, 1)
+    for dx in (-1, 1):
+        @pl.when(twin(dx))
+        def _():
+            p_pass(dx).wait_recv()
+            p_buf[inner[dx]] = p_buf[inner[dx]] + tp_buf[...]
     for d in (-1, 1):
         @pl.when(has("by", d))
         def _():
             p_copy(0, d).start()
     red_own[1] = red_finish(0)
     red_start(1)
-    for dx, dy in SIDES:
-        @pl.when(both(dx, dy))
-        def _():
-            p_copy(-dx, -dy).wait_recv()
+    def p_arrivals(nx, ny):
+        rows = 128 * ny + (128 + 64 * ny) * (nx - 1)
+        group(planes_of(rp_buf, rows), p_send.at[0], p_recv.at[0]).wait_recv()
+
+    counted(p_arrivals)
     for s in range(2):
         xs, xe = slice(R + 8 * s, R + 8 * s + 8), edge[2 * s - 1]
         for h in range(2):
             ys, ye = slice(R + 8 * h, R + 8 * h + 8), edge[2 * h - 1]
             summed = p_buf[xs, ys] + rp_buf[xe, ys] + rp_buf[xs, ye] + rp_buf[xe, ye]
             out[8 * s:8 * s + 8, 8 * h:8 * h + 8, :] = e_buf[xs, ys, :] * summed
-    for dx, dy in SIDES:
-        @pl.when(both(dx, dy))
-        def _():
-            e_copy(dx, dy).wait_send()
-            p_copy(dx, dy).wait_send()
-            h_copy(dx, dy).wait_send()
+    def departures(nx, ny):
+        group(planes_of(e_buf, 128 * (nx + ny) + 64 * nx * ny), e_send.at[0], e_recv.at[0]).wait_send()
+        blocks = 2 * ny + nx * (1 + ny)
+        group(e_buf.at[pl.ds(0, blocks), pl.ds(0, 24)], h_send.at[0], h_recv.at[0]).wait_send()
+        tiles = e_buf.at[pl.ds(0, nx + ny + nx * ny), pl.ds(0, V)]
+        group(tiles, w_send.at[0], w_recv.at[0]).wait_send()
+        rows = 256 + 128 * ny + (128 + 64 * ny) * (nx - 1)
+        group(planes_of(e_buf, rows), p_send.at[0], p_recv.at[0]).wait_send()
+
+    counted(departures)
     for d in (-1, 1):
         @pl.when(has("bz", d))
         def _():
             face_copy(d).wait_send()
+            share_copy(d).wait_send()
             for g in range(V // G):
                 z_copy(g, d).wait_send()
     red_all(0).wait_send()
@@ -553,32 +688,36 @@
             pltpu.VMEM((EX, EY, CZ), F32),
             pltpu.VMEM((V, CX, CY, CZ), F32),
             pltpu.VMEM((V + 1, EX, CY, CZ), F32),
-            pltpu.VMEM((V, EX, CY, CZ), F32),
+            pltpu.VMEM((V + 1, EX, CY, CZ), F32),
             pltpu.VMEM((V + 1, CX, CY, CZ), F32),
             pltpu.VMEM((V, CX, CY, CZ), F32),
             pltpu.VMEM((V, EX, 2 * CY, CZ), BF16),
             pltpu.VMEM((EX, EY, CZ), F32),
             pltpu.VMEM((EX, EY, CZ), F32),
+            pltpu.VMEM((R, EY, CZ), F32),
             pltpu.VMEM((2, 2 * R, CZ), F32),
+            pltpu.VMEM((3, V, CZ), F32),
             pltpu.VMEM((4, 3, 3 * R, CZ), F32),
             pltpu.VMEM((EX, EY, CZ), F32),
             pltpu.VMEM((V, 2 * R, CX * CY), F32),
             pltpu.VMEM((V, 2 * R, CX * CY), F32),
+            pltpu.VMEM((3, 3, V, CZ), F32),
             pltpu.VMEM((1, V), jnp.int32),
             pltpu.VMEM((3, V, T), F32),
             pltpu.VMEM((3 + T, 2 * V, CZ), F32),
             pltpu.VMEM((2, 4 * R, CZ), F32),
             pltpu.VMEM((V, 256, 256), BF16),
-            pltpu.VMEM((V, 192, 256), BF16),
+            pltpu.VMEM((V, 384, 256), BF16),
+            pltpu.VMEM((V, 192, 128), BF16),
             pltpu.VMEM((V, 2 * CY, 256), BF16),
             pltpu.VMEM((3, V, 2 * CY, 256), BF16),
             pltpu.VMEM((3, V, 128, 256), BF16),
-            pltpu.VMEM((V, CX, CY, CZ), F32),
+            pltpu.VMEM((V + 1, CX, CY, CZ), F32),
             pltpu.VMEM((8, CZ), F32),
             pltpu.VMEM((2, 1, CZ), F32),
             pltpu.VMEM((2, 16, 1, CZ), F32),
-            dma((4,)), dma((9,)), dma((9,)), dma((2,)), dma((2,)), dma((9,)), dma((9,)),
-            dma((2, 2)), dma((2, 2)), dma((9,)), dma((9,)), dma((2,)), dma((2,)),
+            dma((4,)), dma((1,)), dma((3,)), dma((1,)), dma((2,)), dma((4,)), dma((4,)), dma((1,)), dma((2,)),
+            dma((2, 2)), dma((2, 2)), dma((1,)), dma((2,)), dma((2,)), dma((2,)),
             pltpu.SemaphoreType.REGULAR((3,)),
         ],
         compiler_params=pltpu.CompilerParams(

time: 28.6 us -> 28.4 us (level)
  no operation moved by 1% of the time
where the time goes in v4:
time: 28.4 us; the launch traced here: 28.3 us
  Pallas kernels  27.6 us (97%)
  local copies, waits for them, and re-layouts  0.66 us (2%)
    pallas_call x1, Pallas kernels, on_device(): pl.pallas_call(kernel, out_shape=jax.ShapeDtypeStruct((CX, CY, CZ), F32),...  27.6 us
    unnamed x1, local copies, waits for them, and re-layouts  0.66 us

profile of v4, /device:TPU:1, one launch (start us, length us, event | category | flops | bytes accessed | tf_op | source)
XLA Modules:
  0.0 28.3 jit_solution(12531286075681336687)
XLA Ops:
  0.0 27.6 %shard_map.46 = f32[16,16,128]{2,1,0:T(8,128)S(1)} custom-call(f32[16,16,128]{2,1,0:T(8,128)} %est.1, f32[8,16,16,128]{3,2,1,0:T(8,128)} %obs.1, s32[1,8]{1,0:T(1,128)} %bitcast.3, f32[3,8,17]{2,1,0:T(8,128)} %bitcast.2), custom_call_target="tpu_custom_call" | custom-call | tf_op jit(solution)/shard_map/pallas_call | solution.py:682
  27.6 0.7 %copy.6 = f32[16,16,128]{2,1,0:T(8,128)} copy(f32[16,16,128]{2,1,0:T(8,128)S(1)} %shard_map.46) | data formatting | bytes 262144

commit v5 on v4

--- a/solution.py
+++ b/solution.py
@@ -189,9 +189,11 @@
 
     def z_copy(g, dz):
         views = pl.ds(G * g, G)
+        bz, n = ids["bz"], sizes["bz"]
+        place = 1 + (bz + 1) // n if dz > 0 else 2 * ((n - bz) // n)
         side = (dz + 1) // 2
         return remote(
-            sb_buf.at[views, rows[dz]], hb_buf.at[views, rows[-dz]],
+            sb_buf.at[views, rows[dz]], hb_buf.at[views, pl.ds(pl.multiple_of(R * place, R), R)],
             zb_send.at[g, side], zb_recv.at[g, 1 - side], at(0, 0, dz),
         )
 
@@ -473,12 +475,10 @@
                 sb_buf[v, 0:R, 128 * h:128 * h + 128] = flipped[CZ - R:]
                 sb_buf[v, R:2 * R, 128 * h:128 * h + 128] = flipped[:R]
         for d in (-1, 1):
-            @pl.when(has("bz", d))
-            def _():
-                z_copy(g, d).start()
+            z_copy(g, d).start()
 
     def halo_rows(g):
-        flat = hb_buf[G * g:G * g + G].reshape(G * 2 * R, CX * CY)
+        flat = hb_buf[G * g:G * g + G, 0:2 * R].reshape(G * 2 * R, CX * CY)
         hi = flat.astype(BF16).astype(F32)
         pair = jnp.concatenate([hi, flat - hi], axis=0)
         pair = jnp.concatenate([pair[:, :128].T, pair[:, 128:].T], axis=0).astype(BF16)
@@ -592,9 +592,7 @@
 
     for g in range(V // G):
         for d in (-1, 1):
-            @pl.when(has("bz", d))
-            def _():
-                z_copy(g, -d).wait_recv()
+            z_copy(g, d).wait_recv()
         halo = halo_rows(g)
         for v in range(G * g, G * g + G):
             g_buf[v] = g_buf[v] + dot(halo, zh_mat[v]).reshape(CX, CY, CZ)
@@ -627,6 +625,8 @@
             @pl.when(cross_both(dx, dy))
             def _():
                 p_copy(dx, dy).start()
+    red_own[1] = red_finish(0)
+    red_start(1)
     lax.fori_loop(0, V, part(backward_x, range(R, R + CX)), 0)
     backward_y(R, 1)
     backward_y(2 * R, 1)
@@ -639,8 +639,6 @@
         @pl.when(has("by", d))
         def _():
             p_copy(0, d).start()
-    red_own[1] = red_finish(0)
-    red_start(1)
     def p_arrivals(nx, ny):
         rows = 128 * ny + (128 + 64 * ny) * (nx - 1)
         group(planes_of(rp_buf, rows), p_send.at[0], p_recv.at[0]).wait_recv()
@@ -667,8 +665,9 @@
         def _():
             face_copy(d).wait_send()
             share_copy(d).wait_send()
-            for g in range(V // G):
-                z_copy(g, d).wait_send()
+    for g in range(V // G):
+        for d in (-1, 1):
+            z_copy(g, d).wait_send()
     red_all(0).wait_send()
     red_all(1).wait_send()
     final = red_finish(1)
@@ -700,7 +699,7 @@
             pltpu.VMEM((4, 3, 3 * R, CZ), F32),
             pltpu.VMEM((EX, EY, CZ), F32),
             pltpu.VMEM((V, 2 * R, CX * CY), F32),
-            pltpu.VMEM((V, 2 * R, CX * CY), F32),
+            pltpu.VMEM((V, 3 * R, CX * CY), F32),
             pltpu.VMEM((3, 3, V, CZ), F32),
             pltpu.VMEM((1, V), jnp.int32),
             pltpu.VMEM((3, V, T), F32),

time: 28.4 us -> 27.8 us (0.979)
  Pallas kernels: 27.6 us -> 26.8 us
    pallas_call x1, Pallas kernels: 27.6 us -> 26.8 us  [on_device(): pl.pallas_call(kernel, out_shape=jax.ShapeDtypeStruct((CX, CY, CZ), F32),...]
where the time goes in v5:
time: 27.8 us; the launch traced here: 27.5 us
  Pallas kernels  26.8 us (96%)
  local copies, waits for them, and re-layouts  0.66 us (2%)
    pallas_call x1, Pallas kernels, on_device(): pl.pallas_call(kernel, out_shape=jax.ShapeDtypeStruct((CX, CY, CZ), F32),...  26.8 us
    unnamed x1, local copies, waits for them, and re-layouts  0.66 us

profile of v5, /device:TPU:1, one launch (start us, length us, event | category | flops | bytes accessed | tf_op | source)
XLA Modules:
  0.0 27.5 jit_solution(17995534207829404724)
XLA Ops:
  0.0 26.8 %shard_map.46 = f32[16,16,128]{2,1,0:T(8,128)S(1)} custom-call(f32[16,16,128]{2,1,0:T(8,128)} %est.1, f32[8,16,16,128]{3,2,1,0:T(8,128)} %obs.1, s32[1,8]{1,0:T(1,128)} %bitcast.3, f32[3,8,17]{2,1,0:T(8,128)} %bitcast.2), custom_call_target="tpu_custom_call" | custom-call | tf_op jit(solution)/shard_map/pallas_call | solution.py:681
  26.8 0.7 %copy.6 = f32[16,16,128]{2,1,0:T(8,128)} copy(f32[16,16,128]{2,1,0:T(8,128)S(1)} %shard_map.46) | data formatting | bytes 262144

commit v6 on v5

--- a/solution.py
+++ b/solution.py
@@ -44,7 +44,7 @@
     est, obs, cov, taps, out,
     e_buf, o_buf, y_buf, m_buf, g_buf, r_buf, x_buf, p_buf, rp_buf, tp_buf,
     zt_buf, share_buf, h_buf, ht_buf, sb_buf, hb_buf, w_buf, c_buf, k_buf, t_buf, l_buf,
-    zf_mat, zm_mat, zh_mat, yf_mat, yw_mat, yb_mat, b_buf, seen_buf, red_own, red_in,
+    zf_mat, zm_mat, zh_mat, xb_mat, xf_mat, yf_mat, yw_mat, yb_mat, b_buf, seen_buf, red_own, red_in,
     load_sem, e_send, e_recv, w_send, w_recv, f_send, f_recv, h_send, h_recv,
     zb_send, zb_recv, p_send, p_recv, red_send, red_recv, met_sem,
 ):
@@ -324,6 +324,24 @@
         zh_mat[v, 64 + top:64 + top + 2 * R] = f_hi
         zh_mat[v, 128 + top:128 + top + 2 * R] = f_lo
 
+    sparse = jnp.zeros((V, CZ), F32)
+    for k in range(T - 1):
+        sparse = sparse + jnp.where(lane8 == 8 * k, t_buf[3 + k, 0:V], 0.0)
+    for v in range(V):
+        turned = pltpu.roll(jnp.broadcast_to(sparse[v:v + 1], (128, 128)), 0, 1, stride=1, stride_axis=0)
+        last = jnp.broadcast_to(t_buf[2 + T, v:v + 1], (128, 128))
+        low = jnp.where(lane >= row, turned, 0.0)
+        high = jnp.where(lane < row, turned, jnp.where(lane == row, last, 0.0))
+        for i, tile in enumerate((low, high)):
+            k_hi, k_lo = split(tile.T)
+            xb_mat[v, 128 * i:128 * i + 128, 0:128] = k_hi
+            xb_mat[v, 128 * i:128 * i + 128, 128:256] = k_hi
+            xb_mat[v, 128 * i:128 * i + 128, 256:384] = k_lo
+        k_hi, k_lo = split(jnp.where(lane < 64, pltpu.roll(low, 64, 1), pltpu.roll(high, 64, 1)))
+        xf_mat[v, :, 0:128] = k_hi
+        xf_mat[v, :, 128:256] = k_hi
+        xf_mat[v, :, 256:384] = k_lo
+
     load_o.wait()
     seen = jnp.zeros((8, CZ), F32)
     for v in range(V):
@@ -425,8 +443,16 @@
                 cols = slice(128 * i, 128 * i + 128)
                 yw_mat[xb, v, :, cols] = yf_mat[v, :, cols] * wide
 
-    own_planes = range(R, R + CX)
-    lax.fori_loop(0, V, part(forward_x, own_planes, True, y_buf, g_buf), 0)
+
+    def own_x(source, to):
+        for v in range(V):
+            pairs = [split(source[v, own, 8 * h:8 * h + 8, :].reshape(128, CZ)) for h in range(2)]
+            data = jnp.concatenate([jnp.concatenate(p, axis=0) for p in pairs], axis=1)
+            full = dot(xf_mat[v, :, 0:256], data) + dot(xf_mat[v, :, 256:384], data[0:128])
+            for h in range(2):
+                to[v, :, 8 * h:8 * h + 8, :] = full[:, h * CZ:(h + 1) * CZ].reshape(CX, 8, CZ)
+
+    own_x(y_buf, g_buf)
     halo_planes = tuple(range(R)) + tuple(range(R + CX, EX))
 
     def masked_y(xb):
@@ -439,7 +465,7 @@
 
     counted(w_arrivals)
     masked_y(1)
-    lax.fori_loop(0, V, part(forward_x, own_planes, True, m_buf, b_buf), 0)
+    own_x(m_buf, b_buf)
     def x_arrivals(nx, ny):
         group(planes_of(e_buf, nx * (128 + 64 * ny)), e_send.at[0], e_recv.at[0]).wait_recv()
         tiles = w_buf.at[pl.ds(0, nx), pl.ds(0, 3)] if ny == 2 else w_buf.at[pl.ds(0, 2), pl.ds(0, nx)]
@@ -574,21 +600,16 @@
             for i in range(2):
                 yb_mat[xb, v, :, 128 * i:128 * i + 128] = pair[i] * w
 
-    def backward_x(outputs, v, carry):
-        t = x_taps(v)
-        for xo in outputs:
-            accs = []
-            for h in range(CY // 8):
-                ys = pl.ds(8 * h, 8)
-                acc = None
-                for xi in range(max(0, xo - T + 1), min(CX, xo + 1)):
-                    term = t[xo - xi] * g_buf[v, xi, ys, :]
-                    acc = term if acc is None else acc + term
-                accs.append(acc)
-            hi, lo = split(jnp.concatenate(accs, axis=0))
-            x_buf[v, xo, 0:CY, :] = hi
-            x_buf[v, xo, CY:2 * CY, :] = lo
-        return carry
+    def backward_x(v):
+        pairs = [split(g_buf[v, :, 8 * h:8 * h + 8, :].reshape(128, CZ)) for h in range(2)]
+        data = jnp.concatenate([jnp.concatenate(p, axis=0) for p in pairs], axis=1)
+        full = dot(xb_mat[v, :, 0:256], data) + dot(xb_mat[v, :, 256:384], data[0:128])
+        planes = jnp.concatenate(
+            [full[:, h * CZ:(h + 1) * CZ].reshape(EX, 8, CZ) for h in range(2)], axis=1
+        )
+        hi, lo = split(planes)
+        x_buf[v, :, 0:CY, :] = hi
+        x_buf[v, :, CY:2 * CY, :] = lo
 
     for g in range(V // G):
         for d in (-1, 1):
@@ -597,7 +618,8 @@
         for v in range(G * g, G * g + G):
             g_buf[v] = g_buf[v] + dot(halo, zh_mat[v]).reshape(CX, CY, CZ)
 
-    lax.fori_loop(0, V, part(backward_x, halo_planes), 0)
+    for v in range(V):
+        backward_x(v)
 
     def backward_y(x0, xb):
         full = None
@@ -625,11 +647,10 @@
             @pl.when(cross_both(dx, dy))
             def _():
                 p_copy(dx, dy).start()
+    backward_y(R, 1)
+    backward_y(2 * R, 1)
     red_own[1] = red_finish(0)
     red_start(1)
-    lax.fori_loop(0, V, part(backward_x, range(R, R + CX)), 0)
-    backward_y(R, 1)
-    backward_y(2 * R, 1)
     for dx in (-1, 1):
         @pl.when(twin(dx))
         def _():
@@ -708,6 +729,8 @@
             pltpu.VMEM((V, 256, 256), BF16),
             pltpu.VMEM((V, 384, 256), BF16),
             pltpu.VMEM((V, 192, 128), BF16),
+            pltpu.VMEM((V, 256, 384), BF16),
+            pltpu.VMEM((V, 128, 384), BF16),
             pltpu.VMEM((V, 2 * CY, 256), BF16),
             pltpu.VMEM((3, V, 2 * CY, 256), BF16),
             pltpu.VMEM((3, V, 128, 256), BF16),

time: 27.8 us -> 26.8 us (0.964)
  Pallas kernels: 26.8 us -> 25.9 us
    pallas_call x1, Pallas kernels: 26.8 us -> 25.9 us  [on_device(): pl.pallas_call(kernel, out_shape=jax.ShapeDtypeStruct((CX, CY, CZ), F32),...]
where the time goes in v6:
time: 26.8 us; the launch traced here: 26.5 us
  Pallas kernels  25.9 us (97%)
  local copies, waits for them, and re-layouts  0.66 us (2%)
    pallas_call x1, Pallas kernels, on_device(): pl.pallas_call(kernel, out_shape=jax.ShapeDtypeStruct((CX, CY, CZ), F32),...  25.9 us
    unnamed x1, local copies, waits for them, and re-layouts  0.66 us

profile of v6, /device:TPU:1, one launch (start us, length us, event | category | flops | bytes accessed | tf_op | source)
XLA Modules:
  0.0 26.5 jit_solution(10471744481169211673)
XLA Ops:
  0.0 25.9 %shard_map.46 = f32[16,16,128]{2,1,0:T(8,128)S(1)} custom-call(f32[16,16,128]{2,1,0:T(8,128)} %est.1, f32[8,16,16,128]{3,2,1,0:T(8,128)} %obs.1, s32[1,8]{1,0:T(1,128)} %bitcast.3, f32[3,8,17]{2,1,0:T(8,128)} %bitcast.2), custom_call_target="tpu_custom_call" | custom-call | tf_op jit(solution)/shard_map/pallas_call | solution.py:702
  25.9 0.7 %copy.6 = f32[16,16,128]{2,1,0:T(8,128)} copy(f32[16,16,128]{2,1,0:T(8,128)S(1)} %shard_map.46) | data formatting | bytes 262144

commit v7 on v6

--- a/solution.py
+++ b/solution.py
@@ -338,9 +338,13 @@
             xb_mat[v, 128 * i:128 * i + 128, 128:256] = k_hi
             xb_mat[v, 128 * i:128 * i + 128, 256:384] = k_lo
         k_hi, k_lo = split(jnp.where(lane < 64, pltpu.roll(low, 64, 1), pltpu.roll(high, 64, 1)))
-        xf_mat[v, :, 0:128] = k_hi
-        xf_mat[v, :, 128:256] = k_hi
-        xf_mat[v, :, 256:384] = k_lo
+        xf_mat[0, v, :, 0:128] = k_hi
+        xf_mat[0, v, :, 128:256] = k_hi
+        xf_mat[0, v, :, 256:384] = k_lo
+        k_hi, k_lo = split(jnp.where(lane < 64, low, high))
+        xf_mat[1, v, :, 0:128] = k_hi
+        xf_mat[1, v, :, 128:256] = k_hi
+        xf_mat[1, v, :, 256:384] = k_lo
 
     load_o.wait()
     seen = jnp.zeros((8, CZ), F32)
@@ -444,15 +448,25 @@
                 yw_mat[xb, v, :, cols] = yf_mat[v, :, cols] * wide
 
 
-    def own_x(source, to):
+    def planes_x(source, to, halo):
         for v in range(V):
-            pairs = [split(source[v, own, 8 * h:8 * h + 8, :].reshape(128, CZ)) for h in range(2)]
-            data = jnp.concatenate([jnp.concatenate(p, axis=0) for p in pairs], axis=1)
-            full = dot(xf_mat[v, :, 0:256], data) + dot(xf_mat[v, :, 256:384], data[0:128])
+            pairs = []
             for h in range(2):
-                to[v, :, 8 * h:8 * h + 8, :] = full[:, h * CZ:(h + 1) * CZ].reshape(CX, 8, CZ)
-
-    own_x(y_buf, g_buf)
+                ys = slice(8 * h, 8 * h + 8)
+                if halo:
+                    f = jnp.concatenate([source[v, 0:R, ys], source[v, EX - R:EX, ys]], axis=0)
+                else:
+                    f = source[v, R:R + CX, ys]
+                pairs.append(jnp.concatenate(split(f.reshape(128, CZ)), axis=0))
+            data = jnp.concatenate(pairs, axis=1)
+            mat = xf_mat.at[halo, v]
+            full = dot(mat[:, 0:256], data) + dot(mat[:, 256:384], data[0:128])
+            for h in range(2):
+                ys = slice(8 * h, 8 * h + 8)
+                f = full[:, h * CZ:(h + 1) * CZ].reshape(CX, 8, CZ)
+                to[v, :, ys, :] = to[v, :, ys, :] + f if halo else f
+
+    planes_x(y_buf, g_buf, 0)
     halo_planes = tuple(range(R)) + tuple(range(R + CX, EX))
 
     def masked_y(xb):
@@ -465,7 +479,7 @@
 
     counted(w_arrivals)
     masked_y(1)
-    own_x(m_buf, b_buf)
+    planes_x(m_buf, b_buf, 0)
     def x_arrivals(nx, ny):
         group(planes_of(e_buf, nx * (128 + 64 * ny)), e_send.at[0], e_recv.at[0]).wait_recv()
         tiles = w_buf.at[pl.ds(0, nx), pl.ds(0, 3)] if ny == 2 else w_buf.at[pl.ds(0, 2), pl.ds(0, nx)]
@@ -474,10 +488,10 @@
     counted(x_arrivals)
     for x0 in (0, 4, EX - 8, EX - 4):
         forward_y(x0)
-    lax.fori_loop(0, V, part(forward_x, halo_planes, False, y_buf, g_buf), 0)
+    planes_x(y_buf, g_buf, 1)
     masked_y(0)
     masked_y(2)
-    lax.fori_loop(0, V, part(forward_x, halo_planes, False, m_buf, b_buf), 0)
+    planes_x(m_buf, b_buf, 1)
     met(met_sem.at[1], ROUNDS[2])
     meet(met_sem.at[2], ROUNDS[3])
 
@@ -730,7 +744,7 @@
             pltpu.VMEM((V, 384, 256), BF16),
             pltpu.VMEM((V, 192, 128), BF16),
             pltpu.VMEM((V, 256, 384), BF16),
-            pltpu.VMEM((V, 128, 384), BF16),
+            pltpu.VMEM((2, V, 128, 384), BF16),
             pltpu.VMEM((V, 2 * CY, 256), BF16),
             pltpu.VMEM((3, V, 2 * CY, 256), BF16),
             pltpu.VMEM((3, V, 128, 256), BF16),

time: 26.8 us -> 26.6 us (level)
  Pallas kernels: 25.9 us -> 25.6 us
where the time goes in v7:
time: 26.6 us; the launch traced here: 26.3 us
  Pallas kernels  25.6 us (96%)
  local copies, waits for them, and re-layouts  0.66 us (2%)
    pallas_call x1, Pallas kernels, on_device(): pl.pallas_call(kernel, out_shape=jax.ShapeDtypeStruct((CX, CY, CZ), F32),...  25.6 us
    unnamed x1, local copies, waits for them, and re-layouts  0.66 us

profile of v7, /device:TPU:1, one launch (start us, length us, event | category | flops | bytes accessed | tf_op | source)
XLA Modules:
  0.0 26.3 jit_solution(15259897100487012372)
XLA Ops:
  0.0 25.6 %shard_map.46 = f32[16,16,128]{2,1,0:T(8,128)S(1)} custom-call(f32[16,16,128]{2,1,0:T(8,128)} %est.1, f32[8,16,16,128]{3,2,1,0:T(8,128)} %obs.1, s32[1,8]{1,0:T(1,128)} %bitcast.3, f32[3,8,17]{2,1,0:T(8,128)} %bitcast.2), custom_call_target="tpu_custom_call" | custom-call | tf_op jit(solution)/shard_map/pallas_call | solution.py:716
  25.6 0.7 %copy.6 = f32[16,16,128]{2,1,0:T(8,128)} copy(f32[16,16,128]{2,1,0:T(8,128)S(1)} %shard_map.46) | data formatting | bytes 262144

commit v8 on v7

--- a/solution.py
+++ b/solution.py
@@ -324,6 +324,26 @@
         zh_mat[v, 64 + top:64 + top + 2 * R] = f_hi
         zh_mat[v, 128 + top:128 + top + 2 * R] = f_lo
 
+    load_o.wait()
+    seen = jnp.zeros((8, CZ), F32)
+    for v in range(V):
+        seen = seen + w_buf[1, 1, v:v + 1] * jnp.sum(o_buf[v].reshape(CX * CY // 8, 8, CZ), axis=0)
+    count_own = jnp.sum(w_buf[1, 1], axis=0, keepdims=True)
+    seen_buf[...] = seen / count_own
+
+    for d in (-1, 1):
+        @pl.when(has("bz", d))
+        def _():
+            face_copy(-d).wait_recv()
+            share_copy(-d).wait_recv()
+    for b in (1, 2):
+        h_buf[b, 1, 2 * R:] = jnp.where(lane8 < CZ // 2, share_buf[0], share_buf[1])
+    met(met_sem.at[0], ROUNDS[1])
+    meet(met_sem.at[1], ROUNDS[2])
+    for dx, dy in SIDES:
+        @pl.when(both(dx, dy))
+        def _():
+            h_copy(dx, dy).start()
     sparse = jnp.zeros((V, CZ), F32)
     for k in range(T - 1):
         sparse = sparse + jnp.where(lane8 == 8 * k, t_buf[3 + k, 0:V], 0.0)
@@ -346,26 +366,6 @@
         xf_mat[1, v, :, 128:256] = k_hi
         xf_mat[1, v, :, 256:384] = k_lo
 
-    load_o.wait()
-    seen = jnp.zeros((8, CZ), F32)
-    for v in range(V):
-        seen = seen + w_buf[1, 1, v:v + 1] * jnp.sum(o_buf[v].reshape(CX * CY // 8, 8, CZ), axis=0)
-    count_own = jnp.sum(w_buf[1, 1], axis=0, keepdims=True)
-    seen_buf[...] = seen / count_own
-
-    for d in (-1, 1):
-        @pl.when(has("bz", d))
-        def _():
-            face_copy(-d).wait_recv()
-            share_copy(-d).wait_recv()
-    for b in (1, 2):
-        h_buf[b, 1, 2 * R:] = jnp.where(lane8 < CZ // 2, share_buf[0], share_buf[1])
-    met(met_sem.at[0], ROUNDS[1])
-    meet(met_sem.at[1], ROUNDS[2])
-    for dx, dy in SIDES:
-        @pl.when(both(dx, dy))
-        def _():
-            h_copy(dx, dy).start()
     for d in (-1, 1):
         @pl.when(has("by", d))
         def _():

time: 26.6 us -> 26.5 us (level)
  no operation moved by 1% of the time
where the time goes in v8:
time: 26.5 us; the launch traced here: 26.3 us
  Pallas kernels  25.6 us (97%)
  local copies, waits for them, and re-layouts  0.66 us (2%)
    pallas_call x1, Pallas kernels, on_device(): pl.pallas_call(kernel, out_shape=jax.ShapeDtypeStruct((CX, CY, CZ), F32),...  25.6 us
    unnamed x1, local copies, waits for them, and re-layouts  0.66 us

profile of v8, /device:TPU:1, one launch (start us, length us, event | category | flops | bytes accessed | tf_op | source)
XLA Modules:
  0.0 26.3 jit_solution(11871095659975450826)
XLA Ops:
  0.0 25.6 %shard_map.46 = f32[16,16,128]{2,1,0:T(8,128)S(1)} custom-call(f32[16,16,128]{2,1,0:T(8,128)} %est.1, f32[8,16,16,128]{3,2,1,0:T(8,128)} %obs.1, s32[1,8]{1,0:T(1,128)} %bitcast.3, f32[3,8,17]{2,1,0:T(8,128)} %bitcast.2), custom_call_target="tpu_custom_call" | custom-call | tf_op jit(solution)/shard_map/pallas_call | solution.py:716
  25.6 0.7 %copy.6 = f32[16,16,128]{2,1,0:T(8,128)} copy(f32[16,16,128]{2,1,0:T(8,128)S(1)} %shard_map.46) | data formatting | bytes 262144
